TPU v7x, 512 devices: a whole 4x8x8 slice. The times are simulated.
512 devices in a mesh: sec: 32 (over y, x), pan: 16 (over z, core).
Axes of the slice: x: 4, y: 8, z: 8, core: 2. Of those that a mesh axis runs over, the one named last changes fastest.
Arguments:
- wave_state: bfloat16 [32, 512, 512], P('sec', 'pan'), may hold values from -6 to 6
- right_blocks: bfloat16 [32, 16, 512, 512], P('sec', None, None, 'pan'), may hold values from -0.25 to 0.25
- left_blocks: bfloat16 [2304, 512, 512], P('sec', 'pan'), may hold values from -0.125 to 0.125
- coupling: bfloat16 [2304], P('sec'), may hold values from -1 to 1
- channel_term: int32 [2304], P('sec'), may hold values from 0 to 15
- channel_out: int32 [2304], P('sec'), may hold values from 0 to 31, as said below
- sector_dims: int32 [32], P('sec'), may hold values from 128 to 512
Outputs:
- applied: float32 [32, 512, 512], P('sec', 'pan')
Inputs may be any that keep to these rules, and one draw needn't show every extreme that they name: `channel_out`: channel c ends in a sector at most two away from the sector c // 72 that it starts from.
All inputs are finite; a program needn't handle non-finite values.
Results may differ from a plain program's by a relative error of at most 0.0041.
Values may be sent and summed in bfloat16 or wider, within the bound.
A program may use at most 64 MiB of HBM per device.

v0:
```python
import jax
import jax.numpy as jnp
from jax import lax
from jax.sharding import PartitionSpec as P


def joined_along(blocks, dim):
    blocks = jnp.moveaxis(blocks, 0, dim)
    dims = blocks.shape
    return blocks.reshape(*dims[:dim], dims[dim] * dims[dim + 1], *dims[dim + 2 :])


def from_everyone(shard, axis):
    count = lax.axis_size(axis)
    return lax.all_to_all(
        jnp.broadcast_to(shard[None], (count, *shard.shape)), axis, 0, 0, tiled=True
    )


def collect(shard, axis, dim):
    return joined_along(from_everyone(shard, axis), dim)


def passed_along(value, axis, steps):
    count = lax.axis_size(axis)
    first, last = (max(0, -steps), min(count, count - steps))
    return lax.ppermute(value, axis, [(source, source + steps) for source in range(first, last)])


def on_device(
    wave_state, right_blocks, left_blocks, coupling, channel_term, channel_out, sector_dims
):
    panel_rows = wave_state.shape[1]
    block_width = wave_state.shape[2]
    term_count = right_blocks.shape[1]
    channels = left_blocks.shape[0]
    sector = lax.axis_index("sec")
    live_dim = sector_dims[0]
    whole_state = collect(wave_state[0], "pan", 0)
    indices = lax.iota(jnp.int32, block_width)
    inside = (indices[:, None] < live_dim) & (indices[None, :] < live_dim)
    masked = jnp.where(inside, whole_state, jnp.zeros((), jnp.bfloat16))
    slot_ids = lax.iota(jnp.int32, 5)
    term_ids = lax.iota(jnp.int32, term_count)
    slot_index = channel_out - sector + 2
    chosen = (slot_index[None, None, :] == slot_ids[:, None, None]) & (
        channel_term[None, None, :] == term_ids[None, :, None]
    )
    weights = jnp.where(chosen, coupling[None, None, :], jnp.zeros((), jnp.bfloat16)).reshape(
        5 * term_count, channels
    )
    combined = jnp.dot(
        weights,
        left_blocks.reshape(channels, panel_rows * block_width),
        preferred_element_type=jnp.float32,
    )
    combined = combined.astype(jnp.bfloat16).reshape(5, term_count, panel_rows, block_width)
    right_full = lax.all_gather(right_blocks[0], "pan", axis=2, tiled=True)
    term_full = jnp.einsum(
        "ik,wkq->wiq", masked, right_full, preferred_element_type=jnp.float32
    ).astype(jnp.bfloat16)
    partial_value = jnp.einsum(
        "jwri,wiq->jrq", combined, term_full, preferred_element_type=jnp.float32
    )
    collected = partial_value[2][None]
    for offset in (-2, -1, 1, 2):
        collected = collected + passed_along(partial_value[offset + 2][None], "sec", offset)
    row_ids = lax.axis_index("pan") * panel_rows + lax.iota(jnp.int32, panel_rows)
    kept_mask = (row_ids[:, None] < live_dim) & (indices[None, :] < live_dim)
    return jnp.where(kept_mask[None], collected, jnp.zeros((), jnp.float32))


def solution(mesh):
    return jax.shard_map(
        on_device,
        mesh=mesh,
        in_specs=(
            P("sec", "pan", None),
            P("sec", None, None, "pan"),
            P("sec", "pan", None),
            P("sec"),
            P("sec"),
            P("sec"),
            P("sec"),
        ),
        out_specs=P("sec", "pan", None),
        check_vma=False,
    )
```

profile of v0, /device:TPU:32, one launch (start us, length us, event | category | flops | bytes accessed | tf_op | source)
XLA Modules:
  0.0 113.4 jit_solution(11130675007976050938)
XLA Ops:
  6.5 0.0 copy-start
  6.5 0.0 copy-start.1
  6.5 0.0 all-gather.3.cloned.1.call-start
  6.5 0.7 all-gather.3.cloned.1.call-update
  7.3 1.6 %broadcast_in_dim.40 = bf16[16,32,512]{2,1,0:T(8,128)(2,1)} broadcast(bf16[32,512]{1,0:T(8,128)(2,1)} %bitcast.48), dimensions={1,2} | broadcast | bytes 557056 | tf_op jit(solution)/shard_map/broadcast_in_dim | solution.py:16
  8.9 10.4 %all-to-all-start = ((bf16[16,32,512]{2,1,0:T(8,128)(2,1)}), bf16[16,32,512]{2,1,0:T(8,128)(2,1)S(1)}, u32[]{:S(2)}, u32[]{:S(2)}) async-start(bf16[16,32,512]{2,1,0:T(8,128)(2,1)} %broadcast_in_dim.40), calls=%async_computation | async-start | bytes 1048576 | tf_op jit(solution)/shard_map/all_to_all | solution.py:15
  19.3 0.7 subtract_add_fusion
  20.6 3.1 %copy.9 = bf16[9,8,32,512]{3,1,2,0:T(8,128)(2,1)S(1)} copy(bf16[9,8,32,512]{3,2,1,0:T(8,128)(2,1)} %bitcast.45) | data formatting | bytes 4718592
  23.7 0.0 copy-done
  23.8 0.0 copy-done.1
  23.8 0.9 convolution_convert_fusion
  24.7 1.0 copy.10
  25.7 10.6 %all-to-all-done = bf16[16,32,512]{2,1,0:T(8,128)(2,1)S(1)} async-done(((bf16[16,32,512]{2,1,0:T(8,128)(2,1)}), bf16[16,32,512]{2,1,0:T(8,128)(2,1)S(1)}, u32[]{:S(2)}, u32[]{:S(2)}) %all-to-all-start) | async-done | bytes 524320 | tf_op jit(solution)/shard_map/all_to_all | solution.py:15
  36.3 39.5 %all-gather.3.cloned.1.call-done = bf16[1,16,512,512]{2,3,1,0:T(8,128)(2,1)} async-done(((bf16[1,16,512,32]{2,3,1,0:T(8,128)(2,1)}), bf16[1,16,512,512]{2,3,1,0:T(8,128)(2,1)}) %all-gather.3.cloned.1.call-update) | async-done | bytes 8388624 | tf_op jit(solution)/shard_map/all_gather | solution.py:58
  75.9 9.5 %fusion.10 = f32[5,32,512]{2,1,0:T(8,128)S(1)} fusion(bf16[1,16,512,512]{2,3,1,0:T(8,128)(2,1)} %all-gather.3.cloned.1.call-done, bf16[512,512]{1,0:T(8,128)(2,1)S(1)} %bitcast.46, pred[512]{0:T(512)(128)(4,1)S(1)} %iota_compare_fusion.2, bf16[5,16,32,512]{3,2,1,0:T(8,128)(2,1)S(1)} %bitcast.44), kind=kOutput, calls=%fused_computation.7 | convolution fusion | flops 5641863168 | bytes 11862528 | tf_op jit(solution)/shard_map/jwri,wiq->jrq/dot_general | solution.py:62
  85.4 4.8 %collective-permute-start = (f32[1,32,512]{2,1,0:T(8,128)S(1)}, f32[1,32,512]{2,1,0:T(8,128)S(1)}, u32[]{:S(2)}, u32[]{:S(2)}) collective-permute-start(f32[1,32,512]{2,1,0:T(8,128)S(1)} %get-tuple-element.5), channel_id=1, source_target_pairs={{32,0},{48,16},{64,32},{80,48},{96,64},{112,80},{128,96},{144,112}... | collective-permute-start | bytes 196616 | tf_op jit(solution)/shard_map/ppermute | solution.py:27
  90.2 3.1 %collective-permute-start.1 = (f32[1,32,512]{2,1,0:T(8,128)S(1)}, f32[1,32,512]{2,1,0:T(8,128)S(1)}, u32[]{:S(2)}, u32[]{:S(2)}) collective-permute-start(f32[1,32,512]{2,1,0:T(8,128)S(1)} %get-tuple-element.8), channel_id=1, source_target_pairs={{16,0},{32,16},{48,32},{64,48},{80,64},{96,80},{112,96},{128,112},... | collective-permute-start | bytes 196616 | tf_op jit(solution)/shard_map/ppermute | solution.py:27
  93.3 2.8 %collective-permute-start.2 = (f32[1,32,512]{2,1,0:T(8,128)S(1)}, f32[1,32,512]{2,1,0:T(8,128)S(1)}, u32[]{:S(2)}, u32[]{:S(2)}) collective-permute-start(f32[1,32,512]{2,1,0:T(8,128)S(1)} %get-tuple-element.7), channel_id=1, source_target_pairs={{0,16},{16,32},{32,48},{48,64},{64,80},{80,96},{96,112},{112,128},... | collective-permute-start | bytes 196616 | tf_op jit(solution)/shard_map/ppermute | solution.py:27
  96.1 2.6 %collective-permute-start.3 = (f32[1,32,512]{2,1,0:T(8,128)S(1)}, f32[1,32,512]{2,1,0:T(8,128)S(1)}, u32[]{:S(2)}, u32[]{:S(2)}) collective-permute-start(f32[1,32,512]{2,1,0:T(8,128)S(1)} %get-tuple-element.6), channel_id=1, source_target_pairs={{0,32},{16,48},{32,64},{48,80},{64,96},{80,112},{96,128},{112,144}... | collective-permute-start | bytes 196616 | tf_op jit(solution)/shard_map/ppermute | solution.py:27
  98.7 0.0 collective-permute-done
  98.7 0.0 collective-permute-done.1
  98.7 4.0 %collective-permute-done.2 = f32[1,32,512]{2,1,0:T(8,128)S(1)} collective-permute-done((f32[1,32,512]{2,1,0:T(8,128)S(1)}, f32[1,32,512]{2,1,0:T(8,128)S(1)}, u32[]{:S(2)}, u32[]{:S(2)}) %collective-permute-start.2) | collective-permute-done | bytes 65568 | tf_op jit(solution)/shard_map/ppermute | solution.py:27
  102.7 3.1 %collective-permute-done.3 = f32[1,32,512]{2,1,0:T(8,128)S(1)} collective-permute-done((f32[1,32,512]{2,1,0:T(8,128)S(1)}, f32[1,32,512]{2,1,0:T(8,128)S(1)}, u32[]{:S(2)}, u32[]{:S(2)}) %collective-permute-start.3) | collective-permute-done | bytes 65568 | tf_op jit(solution)/shard_map/ppermute | solution.py:27
  105.8 0.7 fusion.29
  (6 shorter events, 0.1 us)
Async XLA Ops:
  6.5 17.2 %copy-start = (s32[72]{0:T(128)S(1)}, s32[72]{0:T(128)}, u32[]{:S(2)}) copy-start(s32[72]{0:T(128)} %param.11) | copy-start | bytes 868
  6.5 17.2 %copy-start.1 = (bf16[72]{0:T(256)(128)(2,1)S(1)}, bf16[72]{0:T(256)(128)(2,1)}, u32[]{:S(2)}) copy-start(bf16[72]{0:T(256)(128)(2,1)} %param.10) | copy-start | bytes 436
  6.5 69.3 %all-gather.3.cloned.1.call-start = ((), (), s32[]{:S(2)}) async-start(), calls=%async_computation.1 | async-start | bytes 8912896 | tf_op jit(solution)/shard_map/all_gather | solution.py:58
  8.9 27.5 %all-to-all-start = ((bf16[16,32,512]{2,1,0:T(8,128)(2,1)}), bf16[16,32,512]{2,1,0:T(8,128)(2,1)S(1)}, u32[]{:S(2)}, u32[]{:S(2)}) async-start(bf16[16,32,512]{2,1,0:T(8,128)(2,1)} %broadcast_in_dim.40), calls=%async_computation | async-start | bytes 1048576 | tf_op jit(solution)/shard_map/all_to_all | solution.py:15
  85.4 13.3 %collective-permute-start = (f32[1,32,512]{2,1,0:T(8,128)S(1)}, f32[1,32,512]{2,1,0:T(8,128)S(1)}, u32[]{:S(2)}, u32[]{:S(2)}) collective-permute-start(f32[1,32,512]{2,1,0:T(8,128)S(1)} %get-tuple-element.5), channel_id=1, source_target_pairs={{32,0},{48,16},{64,32},{80,48},{96,64},{112,80},{128,96},{144,112}... | collective-permute-start | bytes 196616 | tf_op jit(solution)/shard_map/ppermute | solution.py:27
  90.2 8.5 %collective-permute-start.1 = (f32[1,32,512]{2,1,0:T(8,128)S(1)}, f32[1,32,512]{2,1,0:T(8,128)S(1)}, u32[]{:S(2)}, u32[]{:S(2)}) collective-permute-start(f32[1,32,512]{2,1,0:T(8,128)S(1)} %get-tuple-element.8), channel_id=1, source_target_pairs={{16,0},{32,16},{48,32},{64,48},{80,64},{96,80},{112,96},{128,112},... | collective-permute-start | bytes 196616 | tf_op jit(solution)/shard_map/ppermute | solution.py:27
  93.3 9.5 %collective-permute-start.2 = (f32[1,32,512]{2,1,0:T(8,128)S(1)}, f32[1,32,512]{2,1,0:T(8,128)S(1)}, u32[]{:S(2)}, u32[]{:S(2)}) collective-permute-start(f32[1,32,512]{2,1,0:T(8,128)S(1)} %get-tuple-element.7), channel_id=1, source_target_pairs={{0,16},{16,32},{32,48},{48,64},{64,80},{80,96},{96,112},{112,128},... | collective-permute-start | bytes 196616 | tf_op jit(solution)/shard_map/ppermute | solution.py:27
  96.1 9.8 %collective-permute-start.3 = (f32[1,32,512]{2,1,0:T(8,128)S(1)}, f32[1,32,512]{2,1,0:T(8,128)S(1)}, u32[]{:S(2)}, u32[]{:S(2)}) collective-permute-start(f32[1,32,512]{2,1,0:T(8,128)S(1)} %get-tuple-element.6), channel_id=1, source_target_pairs={{0,32},{16,48},{32,64},{48,80},{64,96},{80,112},{96,128},{112,144}... | collective-permute-start | bytes 196616 | tf_op jit(solution)/shard_map/ppermute | solution.py:27
Sparse Core Ops, SparseCore 0:
  9.5 66.3 all-gather.2
where the time goes:
time: 114 us; the launch traced here: 113 us
  waiting for transfers between devices  58 us (51%)
  starting transfers between devices  23.7 us (21%)
  between operations  14.2 us (12%)
  matrix products  10.4 us (9%)
  local copies, waits for them, and re-layouts  5.77 us (5%)
  other arithmetic  1.41 us (1%)
    all_gather x1, waiting for transfers between devices, on_device(): right_full = lax.all_gather(right_blocks[0], 'pan', axis=2, tiled=True)  39.5 us
    ppermute x4, starting transfers between devices, passed_along(): lax.ppermute(value, axis, [(source, source + steps) for source in range(f...  13.3 us
    all_to_all x1, waiting for transfers between devices, from_everyone(): lax.all_to_all(jnp.broadcast_to(shard[None], (count, *shard.shape)), axis...  10.6 us
    all_to_all x1, starting transfers between devices, from_everyone(): lax.all_to_all(jnp.broadcast_to(shard[None], (count, *shard.shape)), axis...  10.4 us
    dot_general x1, matrix products, on_device(): jnp.einsum('jwri,wiq->jrq', combined, term_full, preferred_element_type=j...  9.47 us
    ppermute x4, waiting for transfers between devices, passed_along(): lax.ppermute(value, axis, [(source, source + steps) for source in range(f...  7.12 us
    unnamed x6, local copies, waits for them, and re-layouts  4.12 us
  transfers between devices with their start and end apart: 6, of which 4 were waited for; matrix products, arithmetic and copies ran while one was open for 6% of the time, Pallas kernels for 0%

commit v1 on v0

v1 whole, which is shorter than its diff:
```python
import jax
import jax.numpy as jnp
from jax import lax
from jax.experimental import pallas as pl
from jax.experimental.pallas import tpu as pltpu
from jax.sharding import PartitionSpec as P

MESH = pl.DeviceIdType.MESH
F32 = jnp.float32
BF16 = jnp.bfloat16
OFFSETS = (-2, -1, 1, 2)
CHUNKS = 8


def nt_dot(lhs, rhs):
    return lax.dot_general(lhs, rhs, (((1,), (1,)), ((), ())), preferred_element_type=F32)


def kernel(
    state, right, left, coup, term, outc, dims,
    out_ref,
    ring, mbuf, mfull, lbuf, cbuf, xbuf, part, acc4, inbox, last, inlast,
    vcoup, vterm, vout, sdims,
    local_sem, s_send, s_recv, r_send, r_recv, pair_send, pair_recv,
    x_send, x_recv, a_send, a_recv, b_send, b_recv,
):
    sectors = lax.axis_size("sec")
    panels = lax.axis_size("pan")
    ring_size = panels // 2
    terms, cols, width = right.shape
    channels, rows, _ = left.shape
    sec = lax.axis_index("sec")
    pan = lax.axis_index("pan")
    zed = pan // 2
    core = lax.rem(pan, 2)
    partner = pan + 1 - 2 * core
    ahead = lax.rem(pan + 2, panels)
    behind = lax.rem(pan + panels - 2, panels)
    half = rows // 2
    per_chunk = terms // CHUNKS

    def sector_at(offset):
        return lax.rem(sec + offset + sectors, sectors)

    copy_right = pltpu.make_async_copy(right, ring.at[0], local_sem.at[0])
    copy_state = pltpu.make_async_copy(state.at[0], mbuf.at[pan], local_sem.at[1])
    copy_left = [
        pltpu.make_async_copy(left.at[:, pl.ds(g * half, half), :], lbuf.at[g], local_sem.at[2 + g])
        for g in range(2)
    ]
    tables = [
        pltpu.make_async_copy(coup, vcoup, local_sem.at[4]),
        pltpu.make_async_copy(term, vterm, local_sem.at[5]),
        pltpu.make_async_copy(outc, vout, local_sem.at[6]),
        pltpu.make_async_copy(dims, sdims, local_sem.at[7]),
    ]
    copy_state.start()
    copy_right.start()
    for copy in tables:
        copy.start()
    for copy in copy_left:
        copy.start()

    barrier = pltpu.get_barrier_semaphore()
    peers = [(sec, ahead), (sec, behind), (sec, partner)]
    for offset in OFFSETS:
        for other in (pan, partner):
            peers.append((sector_at(offset), other))
    for peer in peers:
        pl.semaphore_signal(barrier, inc=1, device_id=peer, device_id_type=MESH)

    for copy in tables:
        copy.wait()
    live = sdims[0]
    lanes = channels * half
    slot_row = (vout[...] - sec + 2).astype(F32)
    table = jnp.concatenate(
        [slot_row, vterm[...].astype(F32), vcoup[...].astype(F32), jnp.zeros((5, channels), F32)], axis=0
    ).astype(BF16)
    chan_of_lane = lax.broadcasted_iota(jnp.int32, (channels, lanes), 1) // half
    chan = lax.broadcasted_iota(jnp.int32, (channels, lanes), 0)
    spread = jnp.where(chan_of_lane == chan, 1.0, 0.0).astype(BF16)
    wide = jnp.dot(table, spread, preferred_element_type=F32)
    row_in_half = lax.rem(lax.broadcasted_iota(jnp.int32, (1, lanes), 1), half).astype(F32)
    target = (wide[1:2] * 5.0 + wide[0:1]) * float(half) + row_in_half
    weight = wide[2:3]

    pl.semaphore_wait(barrier, len(peers))

    def state_hop(way, dist, part_rows, index):
        sign = 1 if way == 0 else -1
        owner = lax.rem(pan - sign * 2 * (dist - 1) + panels, panels)
        return pltpu.make_async_remote_copy(
            src_ref=mbuf.at[owner, part_rows],
            dst_ref=mbuf.at[owner, part_rows],
            send_sem=s_send.at[way, index],
            recv_sem=s_recv.at[way, index],
            device_id=(sec, ahead if way == 0 else behind),
            device_id_type=MESH,
        )

    def state_arrival(way, dist, part_rows, index):
        sign = 1 if way == 0 else -1
        owner = lax.rem(pan - sign * 2 * dist + 2 * panels, panels)
        return pltpu.make_async_remote_copy(
            src_ref=mbuf.at[owner, part_rows],
            dst_ref=mbuf.at[owner, part_rows],
            send_sem=s_send.at[way, index],
            recv_sem=s_recv.at[way, index],
            device_id=(sec, ahead if way == 0 else behind),
            device_id_type=MESH,
        )

    def state_rows(way, dist):
        if dist < 4:
            return pl.ds(0, rows)
        return pl.ds(way * half, half)

    def slot(way, dist):
        if dist == 0:
            return 0
        return ring_size - dist if way == 0 else dist

    def ring_hop(way, dist, chunk):
        piece = pl.ds(chunk * per_chunk, per_chunk)
        return pltpu.make_async_remote_copy(
            src_ref=ring.at[slot(way, dist - 1), piece],
            dst_ref=ring.at[slot(way, dist), piece],
            send_sem=r_send.at[way, dist - 1, chunk],
            recv_sem=r_recv.at[way, dist - 1, chunk],
            device_id=(sec, ahead if way == 0 else behind),
            device_id_type=MESH,
        )

    def carried(way, dist, chunk):
        return dist < 4 or (chunk < CHUNKS // 2) == (way == 0)

    sends = []

    def go(copy):
        copy.start()
        sends.append(copy)

    def send_state(dist):
        for way in range(2):
            go(state_hop(way, dist, state_rows(way, dist), dist - 1))

    def wait_state(dist):
        for way in range(2):
            state_arrival(way, dist, state_rows(way, dist), dist - 1).wait_recv()

    def send_own(chunks):
        for chunk in chunks:
            for way in range(2):
                go(ring_hop(way, 1, chunk))

    def service(dist, chunks):
        for chunk in chunks:
            for way in range(2):
                if carried(way, dist, chunk):
                    ring_hop(way, dist, chunk).wait_recv()
                    if dist < 4 and carried(way, dist + 1, chunk):
                        go(ring_hop(way, dist + 1, chunk))

    tile = 256

    def combine(step):
        at = lax.broadcasted_iota(jnp.int32, (tile, lanes), 0).astype(F32) + float(step * tile)
        kron = jnp.where(at == target, weight, 0.0).astype(BF16)
        for g in range(2):
            made = jnp.dot(kron, lbuf[g].reshape(lanes, width), preferred_element_type=F32).astype(BF16)
            groups = tile // half
            cbuf[pl.ds(step * groups, groups), g] = made.reshape(groups, half, width)

    copy_state.wait()
    send_state(1)
    copy_right.wait()
    send_own((0, 1))
    for copy in copy_left:
        copy.wait()
    combine(0)
    combine(1)
    wait_state(1)
    send_state(2)
    send_own((2, 3))
    combine(2)
    combine(3)
    wait_state(2)
    send_state(3)
    send_own((4, 5))
    combine(4)
    wait_state(3)
    send_state(4)
    send_own((6, 7))
    service(1, range(0, 2))
    wait_state(4)
    pair = []
    for step in range(ring_size):
        copy = pltpu.make_async_remote_copy(
            src_ref=mbuf.at[2 * step + core],
            dst_ref=mbuf.at[2 * step + core],
            send_sem=pair_send.at[step],
            recv_sem=pair_recv.at[step],
            device_id=(sec, partner),
            device_id_type=MESH,
        )
        pair.append(copy)
        go(copy)
    service(1, range(2, 4))
    for step in range(ring_size):
        pltpu.make_async_remote_copy(
            src_ref=mbuf.at[2 * step + 1 - core],
            dst_ref=mbuf.at[2 * step + 1 - core],
            send_sem=pair_send.at[step],
            recv_sem=pair_recv.at[step],
            device_id=(sec, partner),
            device_id_type=MESH,
        ).wait_recv()

    row_at = lax.broadcasted_iota(jnp.int32, (width, width), 0)
    col_at = lax.broadcasted_iota(jnp.int32, (width, width), 1)
    masked = jnp.where(
        (row_at < live) & (col_at < live), mbuf[...].reshape(width, width), jnp.zeros((), BF16)
    )
    mfull[...] = masked
    group = 4
    x_copies = []
    for step in range(terms // group):
        block = cbuf[pl.ds(step * group * 5, group * 5)].reshape(group * 5 * rows, width)
        made = jnp.dot(block, mfull[...], preferred_element_type=F32).astype(BF16)
        xbuf[pl.ds(step * group, group), core] = made.reshape(group, 5 * rows, width)
        service(1, (4 + step,))
        copy = pltpu.make_async_remote_copy(
            src_ref=xbuf.at[pl.ds(step * group, group), core],
            dst_ref=xbuf.at[pl.ds(step * group, group), core],
            send_sem=x_send.at[step],
            recv_sem=x_recv.at[step],
            device_id=(sec, partner),
            device_id_type=MESH,
        )
        x_copies.append(copy)
        go(copy)

    part[:, :, pl.ds(128, 128)] = jnp.zeros((10, rows, 128), F32)
    service(2, range(0, 2))
    for step in range(terms // group):
        pltpu.make_async_remote_copy(
            src_ref=xbuf.at[pl.ds(step * group, group), 1 - core],
            dst_ref=xbuf.at[pl.ds(step * group, group), 1 - core],
            send_sem=x_send.at[step],
            recv_sem=x_recv.at[step],
            device_id=(sec, partner),
            device_id_type=MESH,
        ).wait_recv()

    def contract(slots, which):
        total = None
        for w in which:
            blocks = [ring[k, w] for k in slots]
            block = blocks[0] if len(blocks) == 1 else jnp.concatenate(blocks, axis=0)
            product = nt_dot(xbuf[w].reshape(10 * rows, width), block)
            total = product if total is None else total + product
        return total

    def place(slots, total):
        for i, k in enumerate(slots):
            part[:, :, pl.ds(k * cols, cols)] = total[:, i * cols : (i + 1) * cols].reshape(10, rows, cols)

    place((0, 1, 7), contract((0, 1, 7), range(terms)))
    service(2, range(2, 8))
    place((2, 6), contract((2, 6), range(terms)))
    service(3, range(0, 8))
    place((3, 5), contract((3, 5), range(terms)))

    def by_final_step(step):
        low = [step * per_chunk + i for i in range(per_chunk)]
        return low + [terms // 2 + w for w in low]

    def final_wait(step):
        ring_hop(0, 4, step).wait_recv()
        ring_hop(1, 4, CHUNKS // 2 + step).wait_recv()

    final_wait(0)
    acc4[...] = contract((4,), by_final_step(0))

    def a_copy(which, j):
        return pltpu.make_async_remote_copy(
            src_ref=part.at[which * 5 + j],
            dst_ref=inbox.at[j, core],
            send_sem=a_send.at[which, j],
            recv_sem=a_recv.at[j, core],
            device_id=(sector_at(j - 2), 2 * zed + which),
            device_id_type=MESH,
        )

    def b_copy(which, j):
        return pltpu.make_async_remote_copy(
            src_ref=last.at[which * 5 + j],
            dst_ref=inlast.at[j, core],
            send_sem=b_send.at[which, j],
            recv_sem=b_recv.at[j, core],
            device_id=(sector_at(j - 2), 2 * zed + which),
            device_id_type=MESH,
        )

    order = [(which, j) for j in (0, 4, 1, 3) for which in (0, 1)]

    def spread_out(maker):
        copies = [maker(which, j) for which, j in order]
        copies.append(maker(1 - core, 2))
        for copy in copies:
            go(copy)

    def arrivals(target_ref, send_sem, recv_sem, source_ref):
        for j, cls in [(j, cls) for j in (0, 1, 3, 4) for cls in (0, 1)] + [(2, 1 - core)]:
            pltpu.make_async_remote_copy(
                src_ref=source_ref.at[0],
                dst_ref=target_ref.at[j, cls],
                send_sem=send_sem.at[0, j],
                recv_sem=recv_sem.at[j, cls],
                device_id=(sec, partner),
                device_id_type=MESH,
            ).wait_recv()

    spread_out(a_copy)
    for step in range(1, CHUNKS // 2 - 1):
        final_wait(step)
        acc4[...] = acc4[...] + contract((4,), by_final_step(step))
    final_wait(CHUNKS // 2 - 1)
    done = acc4[...] + contract((4,), by_final_step(CHUNKS // 2 - 1))
    done = done.reshape(10, rows // 8, 8, cols)
    packed = jnp.concatenate([done[:, i] for i in range(rows // 8)], axis=2)
    last[...] = packed
    spread_out(b_copy)

    arrivals(inbox, a_send, a_recv, part)
    inbox[2, core] = part[core * 5 + 2]
    inlast[2, core] = last[core * 5 + 2]
    sums = []
    for cls in range(2):
        total = inbox[0, cls]
        for j in range(1, 5):
            total = total + inbox[j, cls]
        sums.append(pltpu.roll(total, zed * cols, axis=1))
    pieces = []
    for k in range(ring_size):
        for cls in range(2):
            pieces.append(sums[cls][:, k * cols : (k + 1) * cols])
    early = jnp.concatenate(pieces, axis=1)
    lane = lax.broadcasted_iota(jnp.int32, (rows, width), 1)
    row = lax.broadcasted_iota(jnp.int32, (rows, width), 0) + pan * rows
    keep = (row < live) & (lane < live)
    here = lane // (2 * cols) == lax.rem(zed + 4, ring_size)

    arrivals(inlast, b_send, b_recv, last)
    lasts = []
    for cls in range(2):
        total = inlast[0, cls]
        for j in range(1, 5):
            total = total + inlast[j, cls]
        lasts.append(
            jnp.concatenate([total[:, i * cols : (i + 1) * cols] for i in range(rows // 8)], axis=0)
        )
    late = jnp.concatenate(lasts * (width // (2 * cols)), axis=1)
    out_ref[0] = jnp.where(keep, early + jnp.where(here, late, 0.0), 0.0)
    for copy in sends:
        copy.wait_send()


def on_device(
    wave_state, right_blocks, left_blocks, coupling, channel_term, channel_out, sector_dims
):
    _, rows, width = wave_state.shape
    _, terms, _, cols = right_blocks.shape
    channels = left_blocks.shape[0]
    panels = lax.axis_size("pan")
    ring_size = panels // 2
    half = rows // 2
    right = jnp.swapaxes(right_blocks[0], 1, 2)
    dma = pltpu.SemaphoreType.DMA
    return pl.pallas_call(
        kernel,
        out_shape=jax.ShapeDtypeStruct((1, rows, width), F32),
        in_specs=[pl.BlockSpec(memory_space=pl.ANY)] * 7,
        out_specs=pl.BlockSpec(memory_space=pltpu.VMEM),
        scratch_shapes=[
            pltpu.VMEM((ring_size, terms, cols, width), BF16),
            pltpu.VMEM((panels, rows, width), BF16),
            pltpu.VMEM((width, width), BF16),
            pltpu.VMEM((2, channels, half, width), BF16),
            pltpu.VMEM((5 * terms, 2, half, width), BF16),
            pltpu.VMEM((terms, 2, 5 * rows, width), BF16),
            pltpu.VMEM((10, rows, ring_size * cols), F32),
            pltpu.VMEM((10 * rows, cols), F32),
            pltpu.VMEM((5, 2, rows, ring_size * cols), F32),
            pltpu.VMEM((10, 8, rows // 8 * cols), F32),
            pltpu.VMEM((5, 2, 8, rows // 8 * cols), F32),
            pltpu.VMEM((1, channels), BF16),
            pltpu.VMEM((1, channels), jnp.int32),
            pltpu.VMEM((1, channels), jnp.int32),
            pltpu.SMEM((1,), jnp.int32),
            dma((8,)),
            dma((2, 4)),
            dma((2, 4)),
            dma((2, 4, CHUNKS)),
            dma((2, 4, CHUNKS)),
            dma((ring_size,)),
            dma((ring_size,)),
            dma((4,)),
            dma((4,)),
            dma((2, 5)),
            dma((5, 2)),
            dma((2, 5)),
            dma((5, 2)),
        ],
        compiler_params=pltpu.CompilerParams(
            collective_id=0, has_side_effects=True, vmem_limit_bytes=60 * 1024 * 1024
        ),
        name="sector_step",
    )(
        wave_state,
        right,
        left_blocks,
        coupling[None],
        channel_term[None],
        channel_out[None],
        sector_dims,
    )


def solution(mesh):
    return jax.shard_map(
        on_device,
        mesh=mesh,
        in_specs=(
            P("sec", "pan", None),
            P("sec", None, None, "pan"),
            P("sec", "pan", None),
            P("sec"),
            P("sec"),
            P("sec"),
            P("sec"),
        ),
        out_specs=P("sec", "pan", None),
        check_vma=False,
    )
```

time: 114 us -> 69.8 us (0.61)
  the two profiles are of different devices: /device:TPU:32 before, /device:TPU:1 now
where the time goes in v1:
time: 69.8 us; the launch traced here: 69.6 us
  Pallas kernels  67.5 us (97%)
  local copies, waits for them, and re-layouts  1.47 us (2%)
    pallas_call x1, Pallas kernels, on_device(): pl.pallas_call(kernel, out_shape=jax.ShapeDtypeStruct((1, rows, width), F...  67.5 us
    unnamed x1, local copies, waits for them, and re-layouts  1.47 us

profile of v1, /device:TPU:1, one launch (start us, length us, event | category | flops | bytes accessed | tf_op | source)
XLA Modules:
  0.0 69.6 jit_solution(4386109934046587497)
XLA Ops:
  0.7 67.5 %sector_step.1 = f32[1,32,512]{2,1,0:T(8,128)} custom-call(bf16[1,32,512]{2,1,0:T(8,128)(2,1)} %state.1, bf16[16,32,512]{2,1,0:T(8,128)(2,1)} %bitcast.6, bf16[72,32,512]{2,1,0:T(8,128)(2,1)} %left.1, bf16[1,72]{1,0:T(2,128)(2,1)} %bitcast.7, s32[1,72]{1,0:T(1,128)} %bitcast.8, s32[1,72]{1,0:T(1,128)} %bitcast.9, s32[1]{0:T(128)S(6)} %copy.9.dims), custom_call_target="tpu_custom_call" | custom-call | tf_op jit(solution)/shard_map/sector_step/pallas_call | solution.py:381
  68.1 1.5 %copy.10 = f32[1,32,512]{2,1,0:T(8,128)} copy(f32[1,32,512]{2,1,0:T(8,128)} %sector_step.1) | data formatting | bytes 131072

commit v2 on v1

v2 whole, which is shorter than its diff:
```python
import jax
import jax.numpy as jnp
from jax import lax
from jax.experimental import pallas as pl
from jax.experimental.pallas import tpu as pltpu
from jax.sharding import PartitionSpec as P

MESH = pl.DeviceIdType.MESH
F32 = jnp.float32
BF16 = jnp.bfloat16
OFFSETS = (-2, -1, 1, 2)
CHUNKS = 8


def nt_dot(lhs, rhs):
    return lax.dot_general(lhs, rhs, (((1,), (1,)), ((), ())), preferred_element_type=F32)


def kernel(
    state, right, left, coup, term, outc, dims,
    out_ref,
    ring, mbuf, mfull, lbuf, cbuf, xbuf, part, acc2, acc3, acc4, inbox, mid, inmid, last, inlast,
    vcoup, vterm, vout, sdims,
    local_sem, s_send, s_recv, r_send, r_recv, pair_send, pair_recv,
    x_send, x_recv, a_send, a_recv, m_send, m_recv, b_send, b_recv,
):
    sectors = lax.axis_size("sec")
    panels = lax.axis_size("pan")
    ring_size = panels // 2
    terms, cols, width = right.shape
    channels, rows, _ = left.shape
    sec = lax.axis_index("sec")
    pan = lax.axis_index("pan")
    zed = pan // 2
    core = lax.rem(pan, 2)
    partner = pan + 1 - 2 * core
    ahead = lax.rem(pan + 2, panels)
    behind = lax.rem(pan + panels - 2, panels)
    half = rows // 2
    per_chunk = terms // CHUNKS

    def sector_at(offset):
        return lax.rem(sec + offset + sectors, sectors)

    def has_sector(offset):
        return (sec + offset >= 0) & (sec + offset < sectors)

    copy_right = pltpu.make_async_copy(right, ring.at[0], local_sem.at[0])
    copy_state = pltpu.make_async_copy(state.at[0], mbuf.at[pan], local_sem.at[1])
    copy_left = [
        pltpu.make_async_copy(left.at[:, pl.ds(g * half, half), :], lbuf.at[g], local_sem.at[2 + g])
        for g in range(2)
    ]
    tables = [
        pltpu.make_async_copy(coup, vcoup, local_sem.at[4]),
        pltpu.make_async_copy(term, vterm, local_sem.at[5]),
        pltpu.make_async_copy(outc, vout, local_sem.at[6]),
        pltpu.make_async_copy(dims, sdims, local_sem.at[7]),
    ]
    copy_state.start()
    copy_right.start()
    for copy in tables:
        copy.start()
    for copy in copy_left:
        copy.start()

    barrier = pltpu.get_barrier_semaphore()
    for peer in (ahead, behind, partner):
        pl.semaphore_signal(barrier, inc=1, device_id=(sec, peer), device_id_type=MESH)
    greeted = 3
    for offset in OFFSETS:
        exists = has_sector(offset)
        greeted = greeted + 2 * jnp.where(exists, 1, 0)

        @pl.when(exists)
        def _():
            for other in (pan, partner):
                pl.semaphore_signal(
                    barrier, inc=1, device_id=(sector_at(offset), other), device_id_type=MESH
                )

    with jax.named_scope("barrier"):
        pl.semaphore_wait(barrier, greeted)

    for offset in OFFSETS:

        @pl.when(jnp.logical_not(has_sector(-offset)))
        def _():
            inbox[offset + 2] = jnp.zeros(inbox.shape[1:], F32)
            inmid[offset + 2] = jnp.zeros(inmid.shape[1:], F32)
            inlast[offset + 2] = jnp.zeros(inlast.shape[1:], F32)

    def state_hop(way, dist, part_rows, index):
        sign = 1 if way == 0 else -1
        owner = lax.rem(pan - sign * 2 * (dist - 1) + panels, panels)
        return pltpu.make_async_remote_copy(
            src_ref=mbuf.at[owner, part_rows],
            dst_ref=mbuf.at[owner, part_rows],
            send_sem=s_send.at[way, index],
            recv_sem=s_recv.at[way, index],
            device_id=(sec, ahead if way == 0 else behind),
            device_id_type=MESH,
        )

    def state_arrival(way, dist, part_rows, index):
        sign = 1 if way == 0 else -1
        owner = lax.rem(pan - sign * 2 * dist + 2 * panels, panels)
        return pltpu.make_async_remote_copy(
            src_ref=mbuf.at[owner, part_rows],
            dst_ref=mbuf.at[owner, part_rows],
            send_sem=s_send.at[way, index],
            recv_sem=s_recv.at[way, index],
            device_id=(sec, ahead if way == 0 else behind),
            device_id_type=MESH,
        )

    def state_rows(way, dist):
        if dist < 4:
            return pl.ds(0, rows)
        return pl.ds(way * half, half)

    def slot(way, dist):
        if dist == 0:
            return 0
        return ring_size - dist if way == 0 else dist

    def ring_hop(way, dist, chunk):
        piece = pl.ds(chunk * per_chunk, per_chunk)
        return pltpu.make_async_remote_copy(
            src_ref=ring.at[slot(way, dist - 1), piece],
            dst_ref=ring.at[slot(way, dist), piece],
            send_sem=r_send.at[way, dist - 1, chunk],
            recv_sem=r_recv.at[way, dist - 1, chunk],
            device_id=(sec, ahead if way == 0 else behind),
            device_id_type=MESH,
        )

    def carried(way, dist, chunk):
        return dist < 4 or (chunk < CHUNKS // 2) == (way == 0)

    sends = []

    def go(copy):
        copy.start()
        sends.append(copy)

    def send_state(dist):
        for way in range(2):
            go(state_hop(way, dist, state_rows(way, dist), dist - 1))

    def wait_state(dist):
        for way in range(2):
            state_arrival(way, dist, state_rows(way, dist), dist - 1).wait_recv()

    def send_own(chunks):
        for chunk in chunks:
            for way in range(2):
                go(ring_hop(way, 1, chunk))

    def service(dist, chunks):
        for chunk in chunks:
            for way in range(2):
                if carried(way, dist, chunk):
                    ring_hop(way, dist, chunk).wait_recv()
                    if dist < 4 and carried(way, dist + 1, chunk):
                        go(ring_hop(way, dist + 1, chunk))

    with jax.named_scope("own_state"):
        copy_state.wait()
        send_state(1)
    with jax.named_scope("own_right"):
        copy_right.wait()
        send_own((0, 1))

    for copy in tables:
        copy.wait()
    live = sdims[0, 0]
    lanes = channels * half
    slot_row = (vout[...] - sec + 2).astype(F32)
    table = jnp.concatenate(
        [slot_row, vterm[...].astype(F32), vcoup[...].astype(F32), jnp.zeros((5, channels), F32)], axis=0
    ).astype(BF16)
    chan_of_lane = lax.broadcasted_iota(jnp.int32, (channels, lanes), 1) // half
    chan = lax.broadcasted_iota(jnp.int32, (channels, lanes), 0)
    spread = jnp.where(chan_of_lane == chan, 1.0, 0.0).astype(BF16)
    wide = jnp.dot(table, spread, preferred_element_type=F32)
    row_in_half = lax.rem(lax.broadcasted_iota(jnp.int32, (1, lanes), 1), half).astype(F32)
    target = (wide[1:2] * 5.0 + wide[0:1]) * float(half) + row_in_half
    weight = wide[2:3]

    tile = 256

    def combine(step):
        at = lax.broadcasted_iota(jnp.int32, (tile, lanes), 0).astype(F32) + float(step * tile)
        kron = jnp.where(at == target, weight, 0.0).astype(BF16)
        for g in range(2):
            made = jnp.dot(kron, lbuf[g].reshape(lanes, width), preferred_element_type=F32).astype(BF16)
            groups = tile // half
            cbuf[pl.ds(step * groups, groups), g] = made.reshape(groups, half, width)

    for copy in copy_left:
        copy.wait()
    with jax.named_scope("combine_a"):
        combine(0)
        combine(1)
    with jax.named_scope("hop_1"):
        wait_state(1)
    send_state(2)
    send_own((2, 3))
    combine(2)
    combine(3)
    with jax.named_scope("hop_2"):
        wait_state(2)
    send_state(3)
    send_own((4, 5))
    combine(4)
    with jax.named_scope("hop_3"):
        wait_state(3)
    send_state(4)
    send_own((6, 7))
    service(1, range(0, 2))
    with jax.named_scope("hop_4"):
        wait_state(4)
    pair = []
    for step in range(ring_size):
        copy = pltpu.make_async_remote_copy(
            src_ref=mbuf.at[2 * step + core],
            dst_ref=mbuf.at[2 * step + core],
            send_sem=pair_send.at[step],
            recv_sem=pair_recv.at[step],
            device_id=(sec, partner),
            device_id_type=MESH,
        )
        pair.append(copy)
        go(copy)
    service(1, range(2, 4))
    for step in range(ring_size):
        pltpu.make_async_remote_copy(
            src_ref=mbuf.at[2 * step + 1 - core],
            dst_ref=mbuf.at[2 * step + 1 - core],
            send_sem=pair_send.at[step],
            recv_sem=pair_recv.at[step],
            device_id=(sec, partner),
            device_id_type=MESH,
        ).wait_recv()

    row_at = lax.broadcasted_iota(jnp.int32, (width, width), 0)
    col_at = lax.broadcasted_iota(jnp.int32, (width, width), 1)
    masked = jnp.where(
        (row_at < live) & (col_at < live), mbuf[...].reshape(width, width), jnp.zeros((), BF16)
    )
    mfull[...] = masked
    group = 4
    x_copies = []
    for step in range(terms // group):
        block = cbuf[pl.ds(step * group * 5, group * 5)].reshape(group * 5 * rows, width)
        made = jnp.dot(block, mfull[...], preferred_element_type=F32).astype(BF16)
        xbuf[pl.ds(step * group, group), core] = made.reshape(group, 5 * rows, width)
        service(1, (4 + step,))
        copy = pltpu.make_async_remote_copy(
            src_ref=xbuf.at[pl.ds(step * group, group), core],
            dst_ref=xbuf.at[pl.ds(step * group, group), core],
            send_sem=x_send.at[step],
            recv_sem=x_recv.at[step],
            device_id=(sec, partner),
            device_id_type=MESH,
        )
        x_copies.append(copy)
        go(copy)

    part[...] = jnp.zeros(part.shape, F32)
    for step in range(terms // group):
        pltpu.make_async_remote_copy(
            src_ref=xbuf.at[pl.ds(step * group, group), 1 - core],
            dst_ref=xbuf.at[pl.ds(step * group, group), 1 - core],
            send_sem=x_send.at[step],
            recv_sem=x_recv.at[step],
            device_id=(sec, partner),
            device_id_type=MESH,
        ).wait_recv()

    def contract(slots, which, held):
        blocks = []
        for w in which:
            pieces = [ring[k, w] for k in slots]
            blocks.append(pieces[0] if len(pieces) == 1 else jnp.concatenate(pieces, axis=0))
        totals = []
        for owner in range(2):
            total = None if held is None else held[owner]
            for w, block in zip(which, blocks):
                product = nt_dot(xbuf[w, owner], block)
                total = product if total is None else total + product
            totals.append(total)
        return totals

    def place(slots, totals):
        for owner, total in enumerate(totals):
            for i, k in enumerate(slots):
                piece = total[:, i * cols : (i + 1) * cols].reshape(5, rows, cols)
                part[pl.ds(owner * 5, 5), :, pl.ds(k * cols, cols)] = piece

    def keep_in(acc, totals):
        for owner, total in enumerate(totals):
            acc[owner] = total

    def pack(total):
        total = total.reshape(5, rows // 8, 8, cols)
        return jnp.concatenate([total[:, i] for i in range(rows // 8)], axis=2)

    def unpack(packed):
        return jnp.concatenate([packed[:, i * cols : (i + 1) * cols] for i in range(rows // 8)], axis=0)

    def exchange(source, landing, send_sem, recv_sem):
        def copy_to(which, j):
            return pltpu.make_async_remote_copy(
                src_ref=source.at[which * 5 + j],
                dst_ref=landing.at[j, core],
                send_sem=send_sem.at[which, j],
                recv_sem=recv_sem.at[j, core],
                device_id=(sector_at(j - 2), 2 * zed + which),
                device_id_type=MESH,
            )

        def copy_from(j, cls):
            return pltpu.make_async_remote_copy(
                src_ref=source.at[0],
                dst_ref=landing.at[j, cls],
                send_sem=send_sem.at[0, j],
                recv_sem=recv_sem.at[j, cls],
                device_id=(sec, partner),
                device_id_type=MESH,
            )

        def start():
            for j in (0, 4, 1, 3):

                @pl.when(has_sector(j - 2))
                def _():
                    for which in range(2):
                        copy_to(which, j).start()

            copy_to(1 - core, 2).start()

        def wait_recv():
            for j in (0, 4, 1, 3):

                @pl.when(has_sector(2 - j))
                def _():
                    for cls in range(2):
                        copy_from(j, cls).wait_recv()

            copy_from(2, 1 - core).wait_recv()

        def wait_send():
            for j in (0, 4, 1, 3):

                @pl.when(has_sector(j - 2))
                def _():
                    for which in range(2):
                        copy_to(which, j).wait_send()

            copy_to(1 - core, 2).wait_send()

        return start, wait_recv, wait_send

    def sum_of(landing, cls):
        total = landing[0, cls]
        for j in range(1, 5):
            total = total + landing[j, cls]
        return total

    start_a, recv_a, sent_a = exchange(part, inbox, a_send, a_recv)
    start_m, recv_m, sent_m = exchange(mid, inmid, m_send, m_recv)
    start_b, recv_b, sent_b = exchange(last, inlast, b_send, b_recv)

    def chunk_terms(chunk):
        return range(chunk * per_chunk, (chunk + 1) * per_chunk)

    with jax.named_scope("contract_a"):
        place((0, 1, 7), contract((0, 1, 7), range(terms), None))
    with jax.named_scope("ring_2"):
        for chunk in range(CHUNKS):
            service(2, (chunk,))
            if chunk % 2:
                both = range((chunk - 1) * per_chunk, (chunk + 1) * per_chunk)
                totals = contract((2, 6), both, acc2 if chunk > 1 else None)
                if chunk < CHUNKS - 1:
                    keep_in(acc2, totals)
                else:
                    place((2, 6), totals)
    with jax.named_scope("ring_3"):
        service(3, (0,))
        start_a()
        keep_in(acc3, contract((3, 5), chunk_terms(0), None))
        for chunk in range(1, CHUNKS):
            service(3, (chunk,))
            keep_in(acc3, contract((3, 5), chunk_terms(chunk), acc3))
        for owner in range(2):
            for i in range(2):
                mid[pl.ds(owner * 5, 5), pl.ds(8 * i, 8)] = pack(acc3[owner, :, pl.ds(i * cols, cols)])

    def by_final_step(step):
        low = list(chunk_terms(step))
        return low + [terms // 2 + w for w in low]

    def final_wait(step):
        ring_hop(0, 4, step).wait_recv()
        ring_hop(1, 4, CHUNKS // 2 + step).wait_recv()

    final_wait(0)
    start_m()
    keep_in(acc4, contract((4,), by_final_step(0), None))
    for step in range(1, CHUNKS // 2 - 1):
        final_wait(step)
        keep_in(acc4, contract((4,), by_final_step(step), acc4))
    with jax.named_scope("final_wait"):
        final_wait(CHUNKS // 2 - 1)
    with jax.named_scope("last"):
        totals = contract((4,), by_final_step(CHUNKS // 2 - 1), acc4)
        for owner in range(2):
            last[pl.ds(owner * 5, 5)] = pack(totals[owner])
        start_b()

    recv_a()
    inbox[2, core] = part[core * 5 + 2]
    inmid[2, core] = mid[core * 5 + 2]
    inlast[2, core] = last[core * 5 + 2]
    recv_m()
    sums = []
    for cls in range(2):
        total = sum_of(inbox, cls)
        extra = sum_of(inmid, cls)
        total = jnp.concatenate(
            [
                total[:, : 3 * cols],
                unpack(extra[:8]),
                total[:, 4 * cols : 5 * cols],
                unpack(extra[8:]),
                total[:, 6 * cols :],
            ],
            axis=1,
        )
        sums.append(pltpu.roll(total, zed * cols, axis=1))
    pieces = []
    for k in range(ring_size):
        for cls in range(2):
            pieces.append(sums[cls][:, k * cols : (k + 1) * cols])
    early = jnp.concatenate(pieces, axis=1)
    lane = lax.broadcasted_iota(jnp.int32, (rows, width), 1)
    here = lane // (2 * cols) == lax.rem(zed + 4, ring_size)
    with jax.named_scope("sent"):
        for copy in sends:
            copy.wait_send()
        sent_a()
        sent_m()
        sent_b()
    with jax.named_scope("recv_b"):
        recv_b()
    with jax.named_scope("finish"):
        lasts = [unpack(sum_of(inlast, cls)) for cls in range(2)]
        late = jnp.concatenate(lasts * (width // (2 * cols)), axis=1)
        out_ref[0] = early + jnp.where(here, late, 0.0)


def on_device(
    wave_state, right_blocks, left_blocks, coupling, channel_term, channel_out, sector_dims
):
    _, rows, width = wave_state.shape
    _, terms, _, cols = right_blocks.shape
    channels = left_blocks.shape[0]
    panels = lax.axis_size("pan")
    ring_size = panels // 2
    half = rows // 2
    right = jnp.swapaxes(right_blocks[0], 1, 2)
    dma = pltpu.SemaphoreType.DMA
    applied = pl.pallas_call(
        kernel,
        out_shape=jax.ShapeDtypeStruct((1, rows, width), F32),
        in_specs=[pl.BlockSpec(memory_space=pltpu.HBM)] * 7,
        out_specs=pl.BlockSpec(memory_space=pltpu.VMEM),
        scratch_shapes=[
            pltpu.VMEM((ring_size, terms, cols, width), BF16),
            pltpu.VMEM((panels, rows, width), BF16),
            pltpu.VMEM((width, width), BF16),
            pltpu.VMEM((2, channels, half, width), BF16),
            pltpu.VMEM((5 * terms, 2, half, width), BF16),
            pltpu.VMEM((terms, 2, 5 * rows, width), BF16),
            pltpu.VMEM((10, rows, ring_size * cols), F32),
            pltpu.VMEM((2, 5 * rows, 2 * cols), F32),
            pltpu.VMEM((2, 5 * rows, 2 * cols), F32),
            pltpu.VMEM((2, 5 * rows, cols), F32),
            pltpu.VMEM((5, 2, rows, ring_size * cols), F32),
            pltpu.VMEM((10, 16, rows // 8 * cols), F32),
            pltpu.VMEM((5, 2, 16, rows // 8 * cols), F32),
            pltpu.VMEM((10, 8, rows // 8 * cols), F32),
            pltpu.VMEM((5, 2, 8, rows // 8 * cols), F32),
            pltpu.VMEM((1, channels), BF16),
            pltpu.VMEM((1, channels), jnp.int32),
            pltpu.VMEM((1, channels), jnp.int32),
            pltpu.SMEM((1, 1), jnp.int32),
            dma((8,)),
            dma((2, 4)),
            dma((2, 4)),
            dma((2, 4, CHUNKS)),
            dma((2, 4, CHUNKS)),
            dma((ring_size,)),
            dma((ring_size,)),
            dma((4,)),
            dma((4,)),
            dma((2, 5)),
            dma((5, 2)),
            dma((2, 5)),
            dma((5, 2)),
            dma((2, 5)),
            dma((5, 2)),
        ],
        compiler_params=pltpu.CompilerParams(
            collective_id=0, has_side_effects=True, vmem_limit_bytes=60 * 1024 * 1024
        ),
        name="sector_step",
    )(
        wave_state,
        right,
        left_blocks,
        coupling[None],
        channel_term[None],
        channel_out[None],
        sector_dims[None],
    )
    live = sector_dims[0]
    row_ids = lax.axis_index("pan") * rows + lax.iota(jnp.int32, rows)
    kept_mask = (row_ids[:, None] < live) & (lax.iota(jnp.int32, width)[None, :] < live)
    return jnp.where(kept_mask[None], applied, jnp.zeros((), F32))


def solution(mesh):
    return jax.shard_map(
        on_device,
        mesh=mesh,
        in_specs=(
            P("sec", "pan", None),
            P("sec", None, None, "pan"),
            P("sec", "pan", None),
            P("sec"),
            P("sec"),
            P("sec"),
            P("sec"),
        ),
        out_specs=P("sec", "pan", None),
        check_vma=False,
    )
```

time: 69.8 us -> 66.6 us (0.954); the launches traced: 69.6 us -> 65.4 us
  Pallas kernels: 67.5 us -> 63.2 us
  other arithmetic: 0 us -> 1.56 us
  local copies, waits for them, and re-layouts: 1.47 us -> 0 us
    pallas_call x1, Pallas kernels: 67.5 us -> 63.2 us  [on_device(): pl.pallas_call(kernel, out_shape=jax.ShapeDtypeStruct((1, rows, width), F...]
    select_n x0 -> x1, other arithmetic: none -> 1.55 us  [on_device(): return jnp.where(kept_mask[None], applied, jnp.zeros((), F32))]
    unnamed x1 -> x0, local copies, waits for them, and re-layouts: 1.47 us -> none
where the time goes in v2:
time: 66.6 us; the launch traced here: 65.4 us
  Pallas kernels  63.2 us (95%)
  other arithmetic  1.56 us (2%)
  between operations  0.67 us (1%)
    pallas_call x1, Pallas kernels, on_device(): pl.pallas_call(kernel, out_shape=jax.ShapeDtypeStruct((1, rows, width), F...  63.2 us
    select_n x1, other arithmetic, on_device(): return jnp.where(kept_mask[None], applied, jnp.zeros((), F32))  1.55 us

profile of v2, /device:TPU:1, one launch (start us, length us, event | category | flops | bytes accessed | tf_op | source)
XLA Modules:
  0.0 65.4 jit_solution(16854594804008061078)
XLA Ops:
  0.7 63.2 %sector_step.1 = f32[1,32,512]{2,1,0:T(8,128)} custom-call(bf16[1,32,512]{2,1,0:T(8,128)(2,1)} %state.1, bf16[16,32,512]{2,1,0:T(8,128)(2,1)} %bitcast.11, bf16[72,32,512]{2,1,0:T(8,128)(2,1)} %left.1, bf16[1,72]{1,0:T(2,128)(2,1)} %bitcast.12, s32[1,72]{1,0:T(1,128)} %bitcast.13, s32[1,72]{1,0:T(1,128)} %bitcast.14, s32[1,1]{1,0:T(1,128)} %bitcast.10.dims), custom_call_target="tpu_custom_call" | custom-call | tf_op jit(solution)/shard_map/sector_step/pallas_call | solution.py:476
  63.9 1.5 %and_select_fusion = f32[1,32,512]{2,1,0:T(8,128)} fusion(f32[1,32,512]{2,1,0:T(8,128)} %sector_step.1, pred[512]{0:T(512)(128)(4,1)S(1)} %iota_compare_fusion, pred[32]{0:T(512)(128)(4,1)S(1)} %add_compare_fusion), kind=kLoop, calls=%fused_computation | loop fusion | flops 32768 | bytes 131616 | tf_op jit(solution)/shard_map/jit(_where)/select_n | solution.py:533
  (2 shorter events, 0.0 us)

commit v3 on v2

--- a/solution.py
+++ b/solution.py
@@ -9,7 +9,8 @@
 F32 = jnp.float32
 BF16 = jnp.bfloat16
 OFFSETS = (-2, -1, 1, 2)
-CHUNKS = 8
+CHUNKS = 4
+LAST_CHUNKS = 4
 
 
 def nt_dot(lhs, rhs):
@@ -38,6 +39,7 @@
     behind = lax.rem(pan + panels - 2, panels)
     half = rows // 2
     per_chunk = terms // CHUNKS
+    per_last = terms // 2 // LAST_CHUNKS
 
     def sector_at(offset):
         return lax.rem(sec + offset + sectors, sectors)
@@ -48,22 +50,15 @@
     copy_right = pltpu.make_async_copy(right, ring.at[0], local_sem.at[0])
     copy_state = pltpu.make_async_copy(state.at[0], mbuf.at[pan], local_sem.at[1])
     copy_left = [
-        pltpu.make_async_copy(left.at[:, pl.ds(g * half, half), :], lbuf.at[g], local_sem.at[2 + g])
+        pltpu.make_async_copy(left.at[:, pl.ds(g * half, half), :], lbuf.at[g], local_sem.at[2])
         for g in range(2)
     ]
     tables = [
-        pltpu.make_async_copy(coup, vcoup, local_sem.at[4]),
-        pltpu.make_async_copy(term, vterm, local_sem.at[5]),
-        pltpu.make_async_copy(outc, vout, local_sem.at[6]),
-        pltpu.make_async_copy(dims, sdims, local_sem.at[7]),
+        pltpu.make_async_copy(coup, vcoup, local_sem.at[3]),
+        pltpu.make_async_copy(term, vterm, local_sem.at[4]),
+        pltpu.make_async_copy(outc, vout, local_sem.at[5]),
+        pltpu.make_async_copy(dims, sdims, local_sem.at[6]),
     ]
-    copy_state.start()
-    copy_right.start()
-    for copy in tables:
-        copy.start()
-    for copy in copy_left:
-        copy.start()
-
     barrier = pltpu.get_barrier_semaphore()
     for peer in (ahead, behind, partner):
         pl.semaphore_signal(barrier, inc=1, device_id=(sec, peer), device_id_type=MESH)
@@ -79,6 +74,13 @@
                     barrier, inc=1, device_id=(sector_at(offset), other), device_id_type=MESH
                 )
 
+    copy_state.start()
+    copy_right.start()
+    for copy in tables:
+        copy.start()
+    for copy in copy_left:
+        copy.start()
+
     with jax.named_scope("barrier"):
         pl.semaphore_wait(barrier, greeted)
 
@@ -96,7 +98,7 @@
         return pltpu.make_async_remote_copy(
             src_ref=mbuf.at[owner, part_rows],
             dst_ref=mbuf.at[owner, part_rows],
-            send_sem=s_send.at[way, index],
+            send_sem=s_send.at[way],
             recv_sem=s_recv.at[way, index],
             device_id=(sec, ahead if way == 0 else behind),
             device_id_type=MESH,
@@ -108,7 +110,7 @@
         return pltpu.make_async_remote_copy(
             src_ref=mbuf.at[owner, part_rows],
             dst_ref=mbuf.at[owner, part_rows],
-            send_sem=s_send.at[way, index],
+            send_sem=s_send.at[way],
             recv_sem=s_recv.at[way, index],
             device_id=(sec, ahead if way == 0 else behind),
             device_id_type=MESH,
@@ -125,52 +127,48 @@
         return ring_size - dist if way == 0 else dist
 
     def ring_hop(way, dist, chunk):
-        piece = pl.ds(chunk * per_chunk, per_chunk)
+        if dist < 4:
+            piece = pl.ds(chunk * per_chunk, per_chunk)
+        else:
+            piece = pl.ds(way * (terms // 2) + chunk * per_last, per_last)
         return pltpu.make_async_remote_copy(
             src_ref=ring.at[slot(way, dist - 1), piece],
             dst_ref=ring.at[slot(way, dist), piece],
-            send_sem=r_send.at[way, dist - 1, chunk],
-            recv_sem=r_recv.at[way, dist - 1, chunk],
+            send_sem=r_send.at[way],
+            recv_sem=r_recv.at[way, (dist - 1) * CHUNKS + chunk],
             device_id=(sec, ahead if way == 0 else behind),
             device_id_type=MESH,
         )
 
-    def carried(way, dist, chunk):
-        return dist < 4 or (chunk < CHUNKS // 2) == (way == 0)
-
-    sends = []
-
-    def go(copy):
-        copy.start()
-        sends.append(copy)
-
     def send_state(dist):
         for way in range(2):
-            go(state_hop(way, dist, state_rows(way, dist), dist - 1))
+            state_hop(way, dist, state_rows(way, dist), dist - 1).start()
 
     def wait_state(dist):
         for way in range(2):
             state_arrival(way, dist, state_rows(way, dist), dist - 1).wait_recv()
 
-    def send_own(chunks):
-        for chunk in chunks:
-            for way in range(2):
-                go(ring_hop(way, 1, chunk))
-
-    def service(dist, chunks):
-        for chunk in chunks:
-            for way in range(2):
-                if carried(way, dist, chunk):
-                    ring_hop(way, dist, chunk).wait_recv()
-                    if dist < 4 and carried(way, dist + 1, chunk):
-                        go(ring_hop(way, dist + 1, chunk))
+    def send_own(chunk):
+        for way in range(2):
+            ring_hop(way, 1, chunk).start()
+
+    def service(dist, chunk):
+        for way in range(2):
+            ring_hop(way, dist, chunk).wait_recv()
+            if dist < 3:
+                ring_hop(way, dist + 1, chunk).start()
+            else:
+                for piece in range(LAST_CHUNKS):
+                    first = way * (terms // 2) + piece * per_last
+                    if first // per_chunk == chunk:
+                        ring_hop(way, 4, piece).start()
 
     with jax.named_scope("own_state"):
         copy_state.wait()
         send_state(1)
     with jax.named_scope("own_right"):
         copy_right.wait()
-        send_own((0, 1))
+        send_own(0)
 
     for copy in tables:
         copy.wait()
@@ -198,51 +196,50 @@
             groups = tile // half
             cbuf[pl.ds(step * groups, groups), g] = made.reshape(groups, half, width)
 
-    for copy in copy_left:
-        copy.wait()
+    pltpu.make_async_copy(lbuf, lbuf, local_sem.at[2]).wait()
     with jax.named_scope("combine_a"):
         combine(0)
         combine(1)
     with jax.named_scope("hop_1"):
         wait_state(1)
     send_state(2)
-    send_own((2, 3))
+    send_own(1)
     combine(2)
     combine(3)
     with jax.named_scope("hop_2"):
         wait_state(2)
     send_state(3)
-    send_own((4, 5))
+    send_own(2)
     combine(4)
     with jax.named_scope("hop_3"):
         wait_state(3)
     send_state(4)
-    send_own((6, 7))
-    service(1, range(0, 2))
+    send_own(3)
+    service(1, 0)
     with jax.named_scope("hop_4"):
         wait_state(4)
-    pair = []
-    for step in range(ring_size):
-        copy = pltpu.make_async_remote_copy(
+    def pair_copy(step):
+        return pltpu.make_async_remote_copy(
             src_ref=mbuf.at[2 * step + core],
             dst_ref=mbuf.at[2 * step + core],
-            send_sem=pair_send.at[step],
-            recv_sem=pair_recv.at[step],
+            send_sem=pair_send,
+            recv_sem=pair_recv,
             device_id=(sec, partner),
             device_id_type=MESH,
         )
-        pair.append(copy)
-        go(copy)
-    service(1, range(2, 4))
+
     for step in range(ring_size):
-        pltpu.make_async_remote_copy(
-            src_ref=mbuf.at[2 * step + 1 - core],
-            dst_ref=mbuf.at[2 * step + 1 - core],
-            send_sem=pair_send.at[step],
-            recv_sem=pair_recv.at[step],
-            device_id=(sec, partner),
-            device_id_type=MESH,
-        ).wait_recv()
+        pair_copy(step).start()
+    service(1, 1)
+    pair_all = pltpu.make_async_remote_copy(
+        src_ref=mbuf.at[pl.ds(0, ring_size)],
+        dst_ref=mbuf.at[pl.ds(0, ring_size)],
+        send_sem=pair_send,
+        recv_sem=pair_recv,
+        device_id=(sec, partner),
+        device_id_type=MESH,
+    )
+    pair_all.wait_recv()
 
     row_at = lax.broadcasted_iota(jnp.int32, (width, width), 0)
     col_at = lax.broadcasted_iota(jnp.int32, (width, width), 1)
@@ -251,33 +248,31 @@
     )
     mfull[...] = masked
     group = 4
-    x_copies = []
     for step in range(terms // group):
         block = cbuf[pl.ds(step * group * 5, group * 5)].reshape(group * 5 * rows, width)
         made = jnp.dot(block, mfull[...], preferred_element_type=F32).astype(BF16)
         xbuf[pl.ds(step * group, group), core] = made.reshape(group, 5 * rows, width)
-        service(1, (4 + step,))
-        copy = pltpu.make_async_remote_copy(
+        if step % 2:
+            service(1, 2 + step // 2)
+        pltpu.make_async_remote_copy(
             src_ref=xbuf.at[pl.ds(step * group, group), core],
             dst_ref=xbuf.at[pl.ds(step * group, group), core],
-            send_sem=x_send.at[step],
-            recv_sem=x_recv.at[step],
+            send_sem=x_send,
+            recv_sem=x_recv,
             device_id=(sec, partner),
             device_id_type=MESH,
-        )
-        x_copies.append(copy)
-        go(copy)
+        ).start()
+    x_all = pltpu.make_async_remote_copy(
+        src_ref=xbuf.at[:, core],
+        dst_ref=xbuf.at[:, core],
+        send_sem=x_send,
+        recv_sem=x_recv,
+        device_id=(sec, partner),
+        device_id_type=MESH,
+    )
 
     part[...] = jnp.zeros(part.shape, F32)
-    for step in range(terms // group):
-        pltpu.make_async_remote_copy(
-            src_ref=xbuf.at[pl.ds(step * group, group), 1 - core],
-            dst_ref=xbuf.at[pl.ds(step * group, group), 1 - core],
-            send_sem=x_send.at[step],
-            recv_sem=x_recv.at[step],
-            device_id=(sec, partner),
-            device_id_type=MESH,
-        ).wait_recv()
+    x_all.wait_recv()
 
     def contract(slots, which, held):
         blocks = []
@@ -315,18 +310,18 @@
             return pltpu.make_async_remote_copy(
                 src_ref=source.at[which * 5 + j],
                 dst_ref=landing.at[j, core],
-                send_sem=send_sem.at[which, j],
-                recv_sem=recv_sem.at[j, core],
+                send_sem=send_sem.at[j],
+                recv_sem=recv_sem.at[j],
                 device_id=(sector_at(j - 2), 2 * zed + which),
                 device_id_type=MESH,
             )
 
-        def copy_from(j, cls):
+        def both(j):
             return pltpu.make_async_remote_copy(
-                src_ref=source.at[0],
-                dst_ref=landing.at[j, cls],
-                send_sem=send_sem.at[0, j],
-                recv_sem=recv_sem.at[j, cls],
+                src_ref=source.at[pl.ds(0, 2)],
+                dst_ref=landing.at[j],
+                send_sem=send_sem.at[j],
+                recv_sem=recv_sem.at[j],
                 device_id=(sec, partner),
                 device_id_type=MESH,
             )
@@ -346,18 +341,16 @@
 
                 @pl.when(has_sector(2 - j))
                 def _():
-                    for cls in range(2):
-                        copy_from(j, cls).wait_recv()
-
-            copy_from(2, 1 - core).wait_recv()
+                    both(j).wait_recv()
+
+            copy_to(1 - core, 2).wait_recv()
 
         def wait_send():
             for j in (0, 4, 1, 3):
 
                 @pl.when(has_sector(j - 2))
                 def _():
-                    for which in range(2):
-                        copy_to(which, j).wait_send()
+                    both(j).wait_send()
 
             copy_to(1 - core, 2).wait_send()
 
@@ -380,43 +373,40 @@
         place((0, 1, 7), contract((0, 1, 7), range(terms), None))
     with jax.named_scope("ring_2"):
         for chunk in range(CHUNKS):
-            service(2, (chunk,))
-            if chunk % 2:
-                both = range((chunk - 1) * per_chunk, (chunk + 1) * per_chunk)
-                totals = contract((2, 6), both, acc2 if chunk > 1 else None)
-                if chunk < CHUNKS - 1:
-                    keep_in(acc2, totals)
-                else:
-                    place((2, 6), totals)
+            service(2, chunk)
+            totals = contract((2, 6), chunk_terms(chunk), acc2 if chunk else None)
+            if chunk < CHUNKS - 1:
+                keep_in(acc2, totals)
+            else:
+                place((2, 6), totals)
     with jax.named_scope("ring_3"):
-        service(3, (0,))
-        start_a()
-        keep_in(acc3, contract((3, 5), chunk_terms(0), None))
-        for chunk in range(1, CHUNKS):
-            service(3, (chunk,))
-            keep_in(acc3, contract((3, 5), chunk_terms(chunk), acc3))
+        for chunk in range(CHUNKS):
+            service(3, chunk)
+            if chunk == 0:
+                start_a()
+            keep_in(acc3, contract((3, 5), chunk_terms(chunk), acc3 if chunk else None))
         for owner in range(2):
             for i in range(2):
                 mid[pl.ds(owner * 5, 5), pl.ds(8 * i, 8)] = pack(acc3[owner, :, pl.ds(i * cols, cols)])
 
     def by_final_step(step):
-        low = list(chunk_terms(step))
+        low = list(range(step * per_last, (step + 1) * per_last))
         return low + [terms // 2 + w for w in low]
 
     def final_wait(step):
-        ring_hop(0, 4, step).wait_recv()
-        ring_hop(1, 4, CHUNKS // 2 + step).wait_recv()
+        for way in range(2):
+            ring_hop(way, 4, step).wait_recv()
 
     final_wait(0)
     start_m()
     keep_in(acc4, contract((4,), by_final_step(0), None))
-    for step in range(1, CHUNKS // 2 - 1):
+    for step in range(1, LAST_CHUNKS - 1):
         final_wait(step)
         keep_in(acc4, contract((4,), by_final_step(step), acc4))
     with jax.named_scope("final_wait"):
-        final_wait(CHUNKS // 2 - 1)
+        final_wait(LAST_CHUNKS - 1)
     with jax.named_scope("last"):
-        totals = contract((4,), by_final_step(CHUNKS // 2 - 1), acc4)
+        totals = contract((4,), by_final_step(LAST_CHUNKS - 1), acc4)
         for owner in range(2):
             last[pl.ds(owner * 5, 5)] = pack(totals[owner])
         start_b()
@@ -449,8 +439,25 @@
     lane = lax.broadcasted_iota(jnp.int32, (rows, width), 1)
     here = lane // (2 * cols) == lax.rem(zed + 4, ring_size)
     with jax.named_scope("sent"):
-        for copy in sends:
-            copy.wait_send()
+        for way in range(2):
+            pltpu.make_async_remote_copy(
+                src_ref=mbuf.at[pl.ds(0, 7), pl.ds(0, half)],
+                dst_ref=mbuf.at[pl.ds(0, 7), pl.ds(0, half)],
+                send_sem=s_send.at[way],
+                recv_sem=s_recv.at[way, 0],
+                device_id=(sec, partner),
+                device_id_type=MESH,
+            ).wait_send()
+            pltpu.make_async_remote_copy(
+                src_ref=ring.at[pl.ds(0, 7), pl.ds(0, terms // 2)],
+                dst_ref=ring.at[pl.ds(0, 7), pl.ds(0, terms // 2)],
+                send_sem=r_send.at[way],
+                recv_sem=r_recv.at[way, 0],
+                device_id=(sec, partner),
+                device_id_type=MESH,
+            ).wait_send()
+        pair_all.wait_send()
+        x_all.wait_send()
         sent_a()
         sent_m()
         sent_b()
@@ -498,21 +505,21 @@
             pltpu.VMEM((1, channels), jnp.int32),
             pltpu.VMEM((1, channels), jnp.int32),
             pltpu.SMEM((1, 1), jnp.int32),
-            dma((8,)),
+            dma((7,)),
+            dma((2,)),
             dma((2, 4)),
-            dma((2, 4)),
-            dma((2, 4, CHUNKS)),
-            dma((2, 4, CHUNKS)),
-            dma((ring_size,)),
-            dma((ring_size,)),
-            dma((4,)),
-            dma((4,)),
-            dma((2, 5)),
-            dma((5, 2)),
-            dma((2, 5)),
-            dma((5, 2)),
-            dma((2, 5)),
-            dma((5, 2)),
+            dma((2,)),
+            dma((2, 3 * CHUNKS + LAST_CHUNKS)),
+            dma(()),
+            dma(()),
+            dma(()),
+            dma(()),
+            dma((5,)),
+            dma((5,)),
+            dma((5,)),
+            dma((5,)),
+            dma((5,)),
+            dma((5,)),
         ],
         compiler_params=pltpu.CompilerParams(
             collective_id=0, has_side_effects=True, vmem_limit_bytes=60 * 1024 * 1024

time: 66.6 us -> 65.2 us (0.979)
  Pallas kernels: 63.2 us -> 61.8 us
    pallas_call x1, Pallas kernels: 63.2 us -> 61.8 us  [on_device(): pl.pallas_call(kernel, out_shape=jax.ShapeDtypeStruct((1, rows, width), F...]
where the time goes in v3:
time: 65.2 us; the launch traced here: 64.1 us
  Pallas kernels  61.8 us (95%)
  other arithmetic  1.56 us (2%)
  between operations  0.67 us (1%)
    pallas_call x1, Pallas kernels, on_device(): pl.pallas_call(kernel, out_shape=jax.ShapeDtypeStruct((1, rows, width), F...  61.8 us
    select_n x1, other arithmetic, on_device(): return jnp.where(kept_mask[None], applied, jnp.zeros((), F32))  1.55 us

profile of v3, /device:TPU:1, one launch (start us, length us, event | category | flops | bytes accessed | tf_op | source)
XLA Modules:
  0.0 64.1 jit_solution(15623665972440577805)
XLA Ops:
  0.7 61.8 %sector_step.1 = f32[1,32,512]{2,1,0:T(8,128)} custom-call(bf16[1,32,512]{2,1,0:T(8,128)(2,1)} %state.1, bf16[16,32,512]{2,1,0:T(8,128)(2,1)} %bitcast.11, bf16[72,32,512]{2,1,0:T(8,128)(2,1)} %left.1, bf16[1,72]{1,0:T(2,128)(2,1)} %bitcast.12, s32[1,72]{1,0:T(1,128)} %bitcast.13, s32[1,72]{1,0:T(1,128)} %bitcast.14, s32[1,1]{1,0:T(1,128)} %bitcast.10.dims), custom_call_target="tpu_custom_call" | custom-call | tf_op jit(solution)/shard_map/sector_step/pallas_call | solution.py:483
  62.5 1.5 %and_select_fusion = f32[1,32,512]{2,1,0:T(8,128)} fusion(f32[1,32,512]{2,1,0:T(8,128)} %sector_step.1, pred[512]{0:T(512)(128)(4,1)S(1)} %iota_compare_fusion, pred[32]{0:T(512)(128)(4,1)S(1)} %add_compare_fusion), kind=kLoop, calls=%fused_computation | loop fusion | flops 32768 | bytes 131616 | tf_op jit(solution)/shard_map/jit(_where)/select_n | solution.py:540
  (2 shorter events, 0.0 us)

commit v4 on v3

--- a/solution.py
+++ b/solution.py
@@ -10,7 +10,8 @@
 BF16 = jnp.bfloat16
 OFFSETS = (-2, -1, 1, 2)
 CHUNKS = 4
-LAST_CHUNKS = 4
+LAST_TERMS = (3, 2, 2, 1)
+LAST_CHUNKS = len(LAST_TERMS)
 
 
 def nt_dot(lhs, rhs):
@@ -23,7 +24,7 @@
     ring, mbuf, mfull, lbuf, cbuf, xbuf, part, acc2, acc3, acc4, inbox, mid, inmid, last, inlast,
     vcoup, vterm, vout, sdims,
     local_sem, s_send, s_recv, r_send, r_recv, pair_send, pair_recv,
-    x_send, x_recv, a_send, a_recv, m_send, m_recv, b_send, b_recv,
+    x_send, x_recv, a_send, a_recv, m_send, m_recv, b_send, b_recv, column_sem, ready_sem,
 ):
     sectors = lax.axis_size("sec")
     panels = lax.axis_size("pan")
@@ -39,7 +40,7 @@
     behind = lax.rem(pan + panels - 2, panels)
     half = rows // 2
     per_chunk = terms // CHUNKS
-    per_last = terms // 2 // LAST_CHUNKS
+    last_from = [sum(LAST_TERMS[:i]) for i in range(LAST_CHUNKS)]
 
     def sector_at(offset):
         return lax.rem(sec + offset + sectors, sectors)
@@ -60,14 +61,15 @@
         pltpu.make_async_copy(dims, sdims, local_sem.at[6]),
     ]
     barrier = pltpu.get_barrier_semaphore()
+    first = zed == 0
     for peer in (ahead, behind, partner):
         pl.semaphore_signal(barrier, inc=1, device_id=(sec, peer), device_id_type=MESH)
-    greeted = 3
+    others = 0
     for offset in OFFSETS:
         exists = has_sector(offset)
-        greeted = greeted + 2 * jnp.where(exists, 1, 0)
-
-        @pl.when(exists)
+        others = others + 2 * jnp.where(exists, 1, 0)
+
+        @pl.when(first & exists)
         def _():
             for other in (pan, partner):
                 pl.semaphore_signal(
@@ -82,7 +84,7 @@
         copy.start()
 
     with jax.named_scope("barrier"):
-        pl.semaphore_wait(barrier, greeted)
+        pl.semaphore_wait(barrier, 3 + jnp.where(first, others, 0))
 
     for offset in OFFSETS:
 
@@ -130,7 +132,7 @@
         if dist < 4:
             piece = pl.ds(chunk * per_chunk, per_chunk)
         else:
-            piece = pl.ds(way * (terms // 2) + chunk * per_last, per_last)
+            piece = pl.ds(way * (terms // 2) + last_from[chunk], LAST_TERMS[chunk])
         return pltpu.make_async_remote_copy(
             src_ref=ring.at[slot(way, dist - 1), piece],
             dst_ref=ring.at[slot(way, dist), piece],
@@ -159,8 +161,8 @@
                 ring_hop(way, dist + 1, chunk).start()
             else:
                 for piece in range(LAST_CHUNKS):
-                    first = way * (terms // 2) + piece * per_last
-                    if first // per_chunk == chunk:
+                    end = way * (terms // 2) + last_from[piece] + LAST_TERMS[piece]
+                    if (end - 1) // per_chunk == chunk:
                         ring_hop(way, 4, piece).start()
 
     with jax.named_scope("own_state"):
@@ -230,6 +232,15 @@
 
     for step in range(ring_size):
         pair_copy(step).start()
+    for offset in OFFSETS:
+
+        @pl.when(first & has_sector(offset))
+        def _():
+            for other in (pan, partner):
+                pl.semaphore_signal(
+                    column_sem, inc=1, device_id=(sector_at(offset), other), device_id_type=MESH
+                )
+
     service(1, 1)
     pair_all = pltpu.make_async_remote_copy(
         src_ref=mbuf.at[pl.ds(0, ring_size)],
@@ -271,6 +282,14 @@
         device_id_type=MESH,
     )
 
+    @pl.when(first)
+    def _():
+        pl.semaphore_wait(column_sem, others)
+        for step in range(1, ring_size):
+            pl.semaphore_signal(
+                ready_sem, inc=1, device_id=(sec, 2 * step + core), device_id_type=MESH
+            )
+
     part[...] = jnp.zeros(part.shape, F32)
     x_all.wait_recv()
 
@@ -383,6 +402,11 @@
         for chunk in range(CHUNKS):
             service(3, chunk)
             if chunk == 0:
+
+                @pl.when(jnp.logical_not(first))
+                def _():
+                    pl.semaphore_wait(ready_sem, 1)
+
                 start_a()
             keep_in(acc3, contract((3, 5), chunk_terms(chunk), acc3 if chunk else None))
         for owner in range(2):
@@ -390,7 +414,7 @@
                 mid[pl.ds(owner * 5, 5), pl.ds(8 * i, 8)] = pack(acc3[owner, :, pl.ds(i * cols, cols)])
 
     def by_final_step(step):
-        low = list(range(step * per_last, (step + 1) * per_last))
+        low = list(range(last_from[step], last_from[step] + LAST_TERMS[step]))
         return low + [terms // 2 + w for w in low]
 
     def final_wait(step):
@@ -520,6 +544,8 @@
             dma((5,)),
             dma((5,)),
             dma((5,)),
+            pltpu.SemaphoreType.REGULAR,
+            pltpu.SemaphoreType.REGULAR,
         ],
         compiler_params=pltpu.CompilerParams(
             collective_id=0, has_side_effects=True, vmem_limit_bytes=60 * 1024 * 1024

time: 65.2 us -> 63.4 us (0.972); the launches traced: 64.1 us -> 63.3 us
  Pallas kernels: 61.8 us -> 61 us
    pallas_call x1, Pallas kernels: 61.8 us -> 61 us  [on_device(): pl.pallas_call(kernel, out_shape=jax.ShapeDtypeStruct((1, rows, width), F...]
where the time goes in v4:
time: 63.4 us; the launch traced here: 63.3 us
  Pallas kernels  61 us (96%)
  other arithmetic  1.56 us (2%)
  between operations  0.67 us (1%)
    pallas_call x1, Pallas kernels, on_device(): pl.pallas_call(kernel, out_shape=jax.ShapeDtypeStruct((1, rows, width), F...  61 us
    select_n x1, other arithmetic, on_device(): return jnp.where(kept_mask[None], applied, jnp.zeros((), F32))  1.55 us

profile of v4, /device:TPU:1, one launch (start us, length us, event | category | flops | bytes accessed | tf_op | source)
XLA Modules:
  0.0 63.3 jit_solution(11676396192025151572)
XLA Ops:
  0.7 61.0 %sector_step.1 = f32[1,32,512]{2,1,0:T(8,128)} custom-call(bf16[1,32,512]{2,1,0:T(8,128)(2,1)} %state.1, bf16[16,32,512]{2,1,0:T(8,128)(2,1)} %bitcast.11, bf16[72,32,512]{2,1,0:T(8,128)(2,1)} %left.1, bf16[1,72]{1,0:T(2,128)(2,1)} %bitcast.12, s32[1,72]{1,0:T(1,128)} %bitcast.13, s32[1,72]{1,0:T(1,128)} %bitcast.14, s32[1,1]{1,0:T(1,128)} %bitcast.10.dims), custom_call_target="tpu_custom_call" | custom-call | tf_op jit(solution)/shard_map/sector_step/pallas_call | solution.py:507
  61.7 1.5 %and_select_fusion = f32[1,32,512]{2,1,0:T(8,128)} fusion(f32[1,32,512]{2,1,0:T(8,128)} %sector_step.1, pred[512]{0:T(512)(128)(4,1)S(1)} %iota_compare_fusion, pred[32]{0:T(512)(128)(4,1)S(1)} %add_compare_fusion), kind=kLoop, calls=%fused_computation | loop fusion | flops 32768 | bytes 131616 | tf_op jit(solution)/shard_map/jit(_where)/select_n | solution.py:566
  (2 shorter events, 0.0 us)

commit v5 on v4

--- a/solution.py
+++ b/solution.py
@@ -10,8 +10,10 @@
 BF16 = jnp.bfloat16
 OFFSETS = (-2, -1, 1, 2)
 CHUNKS = 4
-LAST_TERMS = (3, 2, 2, 1)
-LAST_CHUNKS = len(LAST_TERMS)
+LAST_TERMS = (3, 2, 2, 1, 3, 2, 2, 1)
+PIECES = len(LAST_TERMS)
+EARLY = 1
+EARLY_PIECES = 3
 
 
 def nt_dot(lhs, rhs):
@@ -23,7 +25,7 @@
     out_ref,
     ring, mbuf, mfull, lbuf, cbuf, xbuf, part, acc2, acc3, acc4, inbox, mid, inmid, last, inlast,
     vcoup, vterm, vout, sdims,
-    local_sem, s_send, s_recv, r_send, r_recv, pair_send, pair_recv,
+    local_sem, s_send, s_recv, r_send, r_recv, l_send, l_recv, pair_send, pair_recv,
     x_send, x_recv, a_send, a_recv, m_send, m_recv, b_send, b_recv, column_sem, ready_sem,
 ):
     sectors = lax.axis_size("sec")
@@ -40,7 +42,7 @@
     behind = lax.rem(pan + panels - 2, panels)
     half = rows // 2
     per_chunk = terms // CHUNKS
-    last_from = [sum(LAST_TERMS[:i]) for i in range(LAST_CHUNKS)]
+    last_from = [sum(LAST_TERMS[:i]) for i in range(PIECES)]
 
     def sector_at(offset):
         return lax.rem(sec + offset + sectors, sectors)
@@ -90,9 +92,9 @@
 
         @pl.when(jnp.logical_not(has_sector(-offset)))
         def _():
-            inbox[offset + 2] = jnp.zeros(inbox.shape[1:], F32)
-            inmid[offset + 2] = jnp.zeros(inmid.shape[1:], F32)
-            inlast[offset + 2] = jnp.zeros(inlast.shape[1:], F32)
+            inbox[pl.ds(2 * offset + 4, 2)] = jnp.zeros((2, *inbox.shape[1:]), F32)
+            inmid[pl.ds(2 * offset + 4, 2)] = jnp.zeros((2, *inmid.shape[1:]), F32)
+            inlast[pl.ds(2 * offset + 4, 2)] = jnp.zeros((2, *inlast.shape[1:]), F32)
 
     def state_hop(way, dist, part_rows, index):
         sign = 1 if way == 0 else -1
@@ -128,16 +130,21 @@
             return 0
         return ring_size - dist if way == 0 else dist
 
+    def goes(way, piece, target):
+        target = lax.rem(target + ring_size, ring_size)
+        ahead_pieces = jnp.where(target < EARLY, EARLY_PIECES, PIECES // 2)
+        return piece < ahead_pieces if way == 0 else piece >= ahead_pieces
+
     def ring_hop(way, dist, chunk):
         if dist < 4:
             piece = pl.ds(chunk * per_chunk, per_chunk)
         else:
-            piece = pl.ds(way * (terms // 2) + last_from[chunk], LAST_TERMS[chunk])
+            piece = pl.ds(last_from[chunk], LAST_TERMS[chunk])
         return pltpu.make_async_remote_copy(
             src_ref=ring.at[slot(way, dist - 1), piece],
             dst_ref=ring.at[slot(way, dist), piece],
-            send_sem=r_send.at[way],
-            recv_sem=r_recv.at[way, (dist - 1) * CHUNKS + chunk],
+            send_sem=r_send.at[way] if dist < 4 else l_send.at[way, chunk],
+            recv_sem=r_recv.at[way, (dist - 1) * CHUNKS + chunk] if dist < 4 else l_recv.at[chunk],
             device_id=(sec, ahead if way == 0 else behind),
             device_id_type=MESH,
         )
@@ -150,20 +157,28 @@
         for way in range(2):
             state_arrival(way, dist, state_rows(way, dist), dist - 1).wait_recv()
 
+    def hop(dist):
+        for way in (1, 0):
+            state_arrival(way, dist, state_rows(way, dist), dist - 1).wait_recv()
+            state_hop(way, dist + 1, state_rows(way, dist + 1), dist).start()
+            ring_hop(way, 1, dist).start()
+
     def send_own(chunk):
         for way in range(2):
             ring_hop(way, 1, chunk).start()
 
     def service(dist, chunk):
-        for way in range(2):
+        for way in (1, 0):
             ring_hop(way, dist, chunk).wait_recv()
             if dist < 3:
                 ring_hop(way, dist + 1, chunk).start()
             else:
-                for piece in range(LAST_CHUNKS):
-                    end = way * (terms // 2) + last_from[piece] + LAST_TERMS[piece]
-                    if (end - 1) // per_chunk == chunk:
-                        ring_hop(way, 4, piece).start()
+                for piece in range(PIECES):
+                    if (last_from[piece] + LAST_TERMS[piece] - 1) // per_chunk == chunk:
+
+                        @pl.when(goes(way, piece, zed + 1 if way == 0 else zed - 1))
+                        def _():
+                            ring_hop(way, 4, piece).start()
 
     with jax.named_scope("own_state"):
         copy_state.wait()
@@ -171,6 +186,7 @@
     with jax.named_scope("own_right"):
         copy_right.wait()
         send_own(0)
+
 
     for copy in tables:
         copy.wait()
@@ -203,23 +219,18 @@
         combine(0)
         combine(1)
     with jax.named_scope("hop_1"):
-        wait_state(1)
-    send_state(2)
-    send_own(1)
+        hop(1)
     combine(2)
     combine(3)
     with jax.named_scope("hop_2"):
-        wait_state(2)
-    send_state(3)
-    send_own(2)
+        hop(2)
     combine(4)
     with jax.named_scope("hop_3"):
-        wait_state(3)
-    send_state(4)
-    send_own(3)
+        hop(3)
     service(1, 0)
     with jax.named_scope("hop_4"):
         wait_state(4)
+
     def pair_copy(step):
         return pltpu.make_async_remote_copy(
             src_ref=mbuf.at[2 * step + core],
@@ -328,20 +339,10 @@
         def copy_to(which, j):
             return pltpu.make_async_remote_copy(
                 src_ref=source.at[which * 5 + j],
-                dst_ref=landing.at[j, core],
-                send_sem=send_sem.at[j],
-                recv_sem=recv_sem.at[j],
+                dst_ref=landing.at[2 * j + core],
+                send_sem=send_sem,
+                recv_sem=recv_sem,
                 device_id=(sector_at(j - 2), 2 * zed + which),
-                device_id_type=MESH,
-            )
-
-        def both(j):
-            return pltpu.make_async_remote_copy(
-                src_ref=source.at[pl.ds(0, 2)],
-                dst_ref=landing.at[j],
-                send_sem=send_sem.at[j],
-                recv_sem=recv_sem.at[j],
-                device_id=(sec, partner),
                 device_id_type=MESH,
             )
 
@@ -355,30 +356,34 @@
 
             copy_to(1 - core, 2).start()
 
+        def wait_all(wait):
+            for count in (4, 6, 8):
+
+                @pl.when(others == count)
+                def _():
+                    wait(
+                        pltpu.make_async_remote_copy(
+                            src_ref=source.at[pl.ds(0, count + 1)],
+                            dst_ref=landing.at[pl.ds(0, count + 1)],
+                            send_sem=send_sem,
+                            recv_sem=recv_sem,
+                            device_id=(sec, partner),
+                            device_id_type=MESH,
+                        )
+                    )
+
         def wait_recv():
-            for j in (0, 4, 1, 3):
-
-                @pl.when(has_sector(2 - j))
-                def _():
-                    both(j).wait_recv()
-
-            copy_to(1 - core, 2).wait_recv()
+            wait_all(lambda copy: copy.wait_recv())
 
         def wait_send():
-            for j in (0, 4, 1, 3):
-
-                @pl.when(has_sector(j - 2))
-                def _():
-                    both(j).wait_send()
-
-            copy_to(1 - core, 2).wait_send()
+            wait_all(lambda copy: copy.wait_send())
 
         return start, wait_recv, wait_send
 
     def sum_of(landing, cls):
-        total = landing[0, cls]
+        total = landing[cls]
         for j in range(1, 5):
-            total = total + landing[j, cls]
+            total = total + landing[2 * j + cls]
         return total
 
     start_a, recv_a, sent_a = exchange(part, inbox, a_send, a_recv)
@@ -414,31 +419,34 @@
                 mid[pl.ds(owner * 5, 5), pl.ds(8 * i, 8)] = pack(acc3[owner, :, pl.ds(i * cols, cols)])
 
     def by_final_step(step):
-        low = list(range(last_from[step], last_from[step] + LAST_TERMS[step]))
-        return low + [terms // 2 + w for w in low]
+        return [
+            w
+            for piece in (step, PIECES // 2 + step)
+            for w in range(last_from[piece], last_from[piece] + LAST_TERMS[piece])
+        ]
 
     def final_wait(step):
-        for way in range(2):
-            ring_hop(way, 4, step).wait_recv()
+        for piece in (step, PIECES // 2 + step):
+            ring_hop(0, 4, piece).wait_recv()
 
     final_wait(0)
     start_m()
     keep_in(acc4, contract((4,), by_final_step(0), None))
-    for step in range(1, LAST_CHUNKS - 1):
+    for step in range(1, PIECES // 2 - 1):
         final_wait(step)
         keep_in(acc4, contract((4,), by_final_step(step), acc4))
     with jax.named_scope("final_wait"):
-        final_wait(LAST_CHUNKS - 1)
+        final_wait(PIECES // 2 - 1)
     with jax.named_scope("last"):
-        totals = contract((4,), by_final_step(LAST_CHUNKS - 1), acc4)
+        totals = contract((4,), by_final_step(PIECES // 2 - 1), acc4)
         for owner in range(2):
             last[pl.ds(owner * 5, 5)] = pack(totals[owner])
         start_b()
 
     recv_a()
-    inbox[2, core] = part[core * 5 + 2]
-    inmid[2, core] = mid[core * 5 + 2]
-    inlast[2, core] = last[core * 5 + 2]
+    inbox[4 + core] = part[core * 5 + 2]
+    inmid[4 + core] = mid[core * 5 + 2]
+    inlast[4 + core] = last[core * 5 + 2]
     recv_m()
     sums = []
     for cls in range(2):
@@ -473,13 +481,19 @@
                 device_id_type=MESH,
             ).wait_send()
             pltpu.make_async_remote_copy(
-                src_ref=ring.at[pl.ds(0, 7), pl.ds(0, terms // 2)],
-                dst_ref=ring.at[pl.ds(0, 7), pl.ds(0, terms // 2)],
+                src_ref=ring.at[pl.ds(0, 3)],
+                dst_ref=ring.at[pl.ds(0, 3)],
                 send_sem=r_send.at[way],
                 recv_sem=r_recv.at[way, 0],
                 device_id=(sec, partner),
                 device_id_type=MESH,
             ).wait_send()
+            for piece in range(PIECES):
+
+                @pl.when(goes(way, piece, zed + 1 if way == 0 else zed - 1))
+                def _():
+                    ring_hop(way, 4, piece).wait_send()
+
         pair_all.wait_send()
         x_all.wait_send()
         sent_a()
@@ -506,7 +520,7 @@
     dma = pltpu.SemaphoreType.DMA
     applied = pl.pallas_call(
         kernel,
-        out_shape=jax.ShapeDtypeStruct((1, rows, width), F32),
+        out_shape=pltpu.VMEM((1, rows, width), F32),
         in_specs=[pl.BlockSpec(memory_space=pltpu.HBM)] * 7,
         out_specs=pl.BlockSpec(memory_space=pltpu.VMEM),
         scratch_shapes=[
@@ -520,11 +534,11 @@
             pltpu.VMEM((2, 5 * rows, 2 * cols), F32),
             pltpu.VMEM((2, 5 * rows, 2 * cols), F32),
             pltpu.VMEM((2, 5 * rows, cols), F32),
-            pltpu.VMEM((5, 2, rows, ring_size * cols), F32),
+            pltpu.VMEM((10, rows, ring_size * cols), F32),
             pltpu.VMEM((10, 16, rows // 8 * cols), F32),
-            pltpu.VMEM((5, 2, 16, rows // 8 * cols), F32),
+            pltpu.VMEM((10, 16, rows // 8 * cols), F32),
             pltpu.VMEM((10, 8, rows // 8 * cols), F32),
-            pltpu.VMEM((5, 2, 8, rows // 8 * cols), F32),
+            pltpu.VMEM((10, 8, rows // 8 * cols), F32),
             pltpu.VMEM((1, channels), BF16),
             pltpu.VMEM((1, channels), jnp.int32),
             pltpu.VMEM((1, channels), jnp.int32),
@@ -533,17 +547,19 @@
             dma((2,)),
             dma((2, 4)),
             dma((2,)),
-            dma((2, 3 * CHUNKS + LAST_CHUNKS)),
-            dma(()),
-            dma(()),
-            dma(()),
-            dma(()),
-            dma((5,)),
-            dma((5,)),
-            dma((5,)),
-            dma((5,)),
-            dma((5,)),
-            dma((5,)),
+            dma((2, 3 * CHUNKS)),
+            dma((2, PIECES)),
+            dma((PIECES,)),
+            dma(()),
+            dma(()),
+            dma(()),
+            dma(()),
+            dma(()),
+            dma(()),
+            dma(()),
+            dma(()),
+            dma(()),
+            dma(()),
             pltpu.SemaphoreType.REGULAR,
             pltpu.SemaphoreType.REGULAR,
         ],

time: 63.4 us -> 61.5 us (0.970)
  Pallas kernels: 61 us -> 60 us
  other arithmetic: 1.56 us -> 0.72 us
    pallas_call x1, Pallas kernels: 61 us -> 60 us  [on_device(): pl.pallas_call(kernel, out_shape=pltpu.VMEM((1, rows, width), F32), in_sp...]
    select_n x1, other arithmetic: 1.55 us -> 0.71 us  [on_device(): return jnp.where(kept_mask[None], applied, jnp.zeros((), F32))]
where the time goes in v5:
time: 61.5 us; the launch traced here: 61.4 us
  Pallas kernels  60 us (98%)
  other arithmetic  0.72 us (1%)
  between operations  0.67 us (1%)
    pallas_call x1, Pallas kernels, on_device(): pl.pallas_call(kernel, out_shape=pltpu.VMEM((1, rows, width), F32), in_sp...  60 us

profile of v5, /device:TPU:1, one launch (start us, length us, event | category | flops | bytes accessed | tf_op | source)
XLA Modules:
  0.0 61.4 jit_solution(18179410791655327483)
XLA Ops:
  0.7 60.0 %sector_step.1 = f32[1,32,512]{2,1,0:T(8,128)S(1)} custom-call(bf16[1,32,512]{2,1,0:T(8,128)(2,1)} %state.1, bf16[16,32,512]{2,1,0:T(8,128)(2,1)} %bitcast.11, bf16[72,32,512]{2,1,0:T(8,128)(2,1)} %left.1, bf16[1,72]{1,0:T(2,128)(2,1)} %bitcast.12, s32[1,72]{1,0:T(1,128)} %bitcast.13, s32[1,72]{1,0:T(1,128)} %bitcast.14, s32[1,1]{1,0:T(1,128)} %bitcast.10.dims), custom_call_target="tpu_custom_call" | custom-call | tf_op jit(solution)/shard_map/sector_step/pallas_call | solution.py:521
  60.7 0.7 %and_select_fusion = f32[1,32,512]{2,1,0:T(8,128)} fusion(f32[1,32,512]{2,1,0:T(8,128)S(1)} %sector_step.1, pred[512]{0:T(512)(128)(4,1)S(1)} %iota_compare_fusion, pred[32]{0:T(512)(128)(4,1)S(1)} %add_compare_fusion), kind=kLoop, calls=%fused_computation | loop fusion | flops 32768 | bytes 131616 | tf_op jit(solution)/shard_map/jit(_where)/select_n | solution.py:582
  (2 shorter events, 0.0 us)

commit v6 on v5

--- a/solution.py
+++ b/solution.py
@@ -12,8 +12,7 @@
 CHUNKS = 4
 LAST_TERMS = (3, 2, 2, 1, 3, 2, 2, 1)
 PIECES = len(LAST_TERMS)
-EARLY = 1
-EARLY_PIECES = 3
+EARLY_PIECES = (2, 3)
 
 
 def nt_dot(lhs, rhs):
@@ -132,7 +131,9 @@
 
     def goes(way, piece, target):
         target = lax.rem(target + ring_size, ring_size)
-        ahead_pieces = jnp.where(target < EARLY, EARLY_PIECES, PIECES // 2)
+        ahead_pieces = PIECES // 2
+        for place, pieces in enumerate(EARLY_PIECES):
+            ahead_pieces = jnp.where(target == place, pieces, ahead_pieces)
         return piece < ahead_pieces if way == 0 else piece >= ahead_pieces
 
     def ring_hop(way, dist, chunk):
@@ -143,7 +144,7 @@
         return pltpu.make_async_remote_copy(
             src_ref=ring.at[slot(way, dist - 1), piece],
             dst_ref=ring.at[slot(way, dist), piece],
-            send_sem=r_send.at[way] if dist < 4 else l_send.at[way, chunk],
+            send_sem=r_send.at[way] if dist < 4 else l_send.at[way],
             recv_sem=r_recv.at[way, (dist - 1) * CHUNKS + chunk] if dist < 4 else l_recv.at[chunk],
             device_id=(sec, ahead if way == 0 else behind),
             device_id_type=MESH,
@@ -157,18 +158,31 @@
         for way in range(2):
             state_arrival(way, dist, state_rows(way, dist), dist - 1).wait_recv()
 
-    def hop(dist):
-        for way in (1, 0):
-            state_arrival(way, dist, state_rows(way, dist), dist - 1).wait_recv()
-            state_hop(way, dist + 1, state_rows(way, dist + 1), dist).start()
+    def hop(dist, way):
+        state_arrival(way, dist, state_rows(way, dist), dist - 1).wait_recv()
+        state_hop(way, dist + 1, state_rows(way, dist + 1), dist).start()
+        if way == 0:
             ring_hop(way, 1, dist).start()
+        else:
+
+            @pl.when(jnp.logical_not(leads))
+            def _():
+                ring_hop(way, 1, dist).start()
+
+            if dist + 1 < CHUNKS:
+
+                @pl.when(leads)
+                def _():
+                    ring_hop(way, 1, dist + 1).start()
+
+    leads = (zed == 1) | (zed == 2)
 
     def send_own(chunk):
         for way in range(2):
             ring_hop(way, 1, chunk).start()
 
-    def service(dist, chunk):
-        for way in (1, 0):
+    def service(dist, chunk, ways=(1, 0)):
+        for way in ways:
             ring_hop(way, dist, chunk).wait_recv()
             if dist < 3:
                 ring_hop(way, dist + 1, chunk).start()
@@ -186,6 +200,10 @@
     with jax.named_scope("own_right"):
         copy_right.wait()
         send_own(0)
+
+        @pl.when(leads)
+        def _():
+            ring_hop(1, 1, 1).start()
 
 
     for copy in tables:
@@ -219,15 +237,21 @@
         combine(0)
         combine(1)
     with jax.named_scope("hop_1"):
-        hop(1)
+        hop(1, 1)
+        hop(1, 0)
     combine(2)
     combine(3)
     with jax.named_scope("hop_2"):
-        hop(2)
+        hop(2, 1)
+        hop(2, 0)
     combine(4)
     with jax.named_scope("hop_3"):
-        hop(3)
-    service(1, 0)
+        hop(3, 1)
+        service(1, 0, (1,))
+        service(1, 1, (1,))
+        hop(3, 0)
+    service(1, 0, (0,))
+    service(1, 1, (0,))
     with jax.named_scope("hop_4"):
         wait_state(4)
 
@@ -252,7 +276,6 @@
                     column_sem, inc=1, device_id=(sector_at(offset), other), device_id_type=MESH
                 )
 
-    service(1, 1)
     pair_all = pltpu.make_async_remote_copy(
         src_ref=mbuf.at[pl.ds(0, ring_size)],
         dst_ref=mbuf.at[pl.ds(0, ring_size)],
@@ -488,11 +511,21 @@
                 device_id=(sec, partner),
                 device_id_type=MESH,
             ).wait_send()
-            for piece in range(PIECES):
-
-                @pl.when(goes(way, piece, zed + 1 if way == 0 else zed - 1))
+            reached = lax.rem(zed + (1 if way == 0 else ring_size - 1), ring_size)
+            for place, ahead_pieces in enumerate((*EARLY_PIECES, PIECES // 2)):
+                is_target = reached == place if place < len(EARLY_PIECES) else reached >= place
+                count = sum(LAST_TERMS[:ahead_pieces] if way == 0 else LAST_TERMS[ahead_pieces:])
+
+                @pl.when(is_target)
                 def _():
-                    ring_hop(way, 4, piece).wait_send()
+                    pltpu.make_async_remote_copy(
+                        src_ref=ring.at[0, pl.ds(0, count)],
+                        dst_ref=ring.at[0, pl.ds(0, count)],
+                        send_sem=l_send.at[way],
+                        recv_sem=l_recv.at[0],
+                        device_id=(sec, partner),
+                        device_id_type=MESH,
+                    ).wait_send()
 
         pair_all.wait_send()
         x_all.wait_send()
@@ -548,7 +581,7 @@
             dma((2, 4)),
             dma((2,)),
             dma((2, 3 * CHUNKS)),
-            dma((2, PIECES)),
+            dma((2,)),
             dma((PIECES,)),
             dma(()),
             dma(()),

time: 61.5 us -> 60.5 us (0.984)
  Pallas kernels: 60 us -> 58.9 us
    pallas_call x1, Pallas kernels: 60 us -> 58.9 us  [on_device(): pl.pallas_call(kernel, out_shape=pltpu.VMEM((1, rows, width), F32), in_sp...]
where the time goes in v6:
time: 60.5 us; the launch traced here: 60.3 us
  Pallas kernels  58.9 us (97%)
  other arithmetic  0.72 us (1%)
  between operations  0.67 us (1%)
    pallas_call x1, Pallas kernels, on_device(): pl.pallas_call(kernel, out_shape=pltpu.VMEM((1, rows, width), F32), in_sp...  58.9 us

profile of v6, /device:TPU:1, one launch (start us, length us, event | category | flops | bytes accessed | tf_op | source)
XLA Modules:
  0.0 60.3 jit_solution(11678807869160569603)
XLA Ops:
  0.7 58.9 %sector_step.1 = f32[1,32,512]{2,1,0:T(8,128)S(1)} custom-call(bf16[1,32,512]{2,1,0:T(8,128)(2,1)} %state.1, bf16[16,32,512]{2,1,0:T(8,128)(2,1)} %bitcast.11, bf16[72,32,512]{2,1,0:T(8,128)(2,1)} %left.1, bf16[1,72]{1,0:T(2,128)(2,1)} %bitcast.12, s32[1,72]{1,0:T(1,128)} %bitcast.13, s32[1,72]{1,0:T(1,128)} %bitcast.14, s32[1,1]{1,0:T(1,128)} %bitcast.10.dims), custom_call_target="tpu_custom_call" | custom-call | tf_op jit(solution)/shard_map/sector_step/pallas_call | solution.py:554
  59.6 0.7 %and_select_fusion = f32[1,32,512]{2,1,0:T(8,128)} fusion(f32[1,32,512]{2,1,0:T(8,128)S(1)} %sector_step.1, pred[512]{0:T(512)(128)(4,1)S(1)} %iota_compare_fusion, pred[32]{0:T(512)(128)(4,1)S(1)} %add_compare_fusion), kind=kLoop, calls=%fused_computation | loop fusion | flops 32768 | bytes 131616 | tf_op jit(solution)/shard_map/jit(_where)/select_n | solution.py:615
  (2 shorter events, 0.0 us)

commit v7 on v6

--- a/solution.py
+++ b/solution.py
@@ -25,7 +25,7 @@
     ring, mbuf, mfull, lbuf, cbuf, xbuf, part, acc2, acc3, acc4, inbox, mid, inmid, last, inlast,
     vcoup, vterm, vout, sdims,
     local_sem, s_send, s_recv, r_send, r_recv, l_send, l_recv, pair_send, pair_recv,
-    x_send, x_recv, a_send, a_recv, m_send, m_recv, b_send, b_recv, column_sem, ready_sem,
+    x_send, x_recv, a_send, a_recv, m_send, m_recv, b_send, b_recv, column_sem, ready_sem, later_sem,
 ):
     sectors = lax.axis_size("sec")
     panels = lax.axis_size("pan")
@@ -63,8 +63,19 @@
     ]
     barrier = pltpu.get_barrier_semaphore()
     first = zed == 0
-    for peer in (ahead, behind, partner):
-        pl.semaphore_signal(barrier, inc=1, device_id=(sec, peer), device_id_type=MESH)
+    pl.semaphore_signal(barrier, inc=1, device_id=(sec, partner), device_id_type=MESH)
+
+    tells_ahead = zed == ring_size - 1
+    tells_behind = zed == 2
+
+    @pl.when(jnp.logical_not(tells_ahead))
+    def _():
+        pl.semaphore_signal(barrier, inc=1, device_id=(sec, ahead), device_id_type=MESH)
+
+    @pl.when(jnp.logical_not(tells_behind))
+    def _():
+        pl.semaphore_signal(barrier, inc=1, device_id=(sec, behind), device_id_type=MESH)
+
     others = 0
     for offset in OFFSETS:
         exists = has_sector(offset)
@@ -85,7 +96,16 @@
         copy.start()
 
     with jax.named_scope("barrier"):
-        pl.semaphore_wait(barrier, 3 + jnp.where(first, others, 0))
+        pl.semaphore_wait(barrier, 3 - jnp.where(zed < 2, 1, 0) + jnp.where(first, others, 0))
+
+    @pl.when(tells_ahead)
+    def _():
+        pl.semaphore_signal(later_sem, inc=1, device_id=(sec, ahead), device_id_type=MESH)
+
+    @pl.when(tells_behind)
+    def _():
+        pl.semaphore_signal(later_sem, inc=1, device_id=(sec, behind), device_id_type=MESH)
+
 
     for offset in OFFSETS:
 
@@ -194,17 +214,35 @@
                         def _():
                             ring_hop(way, 4, piece).start()
 
+    def first_sends(way):
+        state_hop(way, 1, state_rows(way, 1), 0).start()
+        ring_hop(way, 1, 0).start()
+        if way == 1:
+
+            @pl.when(leads)
+            def _():
+                ring_hop(1, 1, 1).start()
+
     with jax.named_scope("own_state"):
         copy_state.wait()
-        send_state(1)
-    with jax.named_scope("own_right"):
         copy_right.wait()
-        send_own(0)
-
-        @pl.when(leads)
-        def _():
-            ring_hop(1, 1, 1).start()
-
+
+    @pl.when(zed == 0)
+    def _():
+        first_sends(0)
+        pl.semaphore_wait(later_sem, 1)
+        first_sends(1)
+
+    @pl.when(zed == 1)
+    def _():
+        first_sends(1)
+        pl.semaphore_wait(later_sem, 1)
+        first_sends(0)
+
+    @pl.when(zed > 1)
+    def _():
+        first_sends(1)
+        first_sends(0)
 
     for copy in tables:
         copy.wait()
@@ -595,6 +633,7 @@
             dma(()),
             pltpu.SemaphoreType.REGULAR,
             pltpu.SemaphoreType.REGULAR,
+            pltpu.SemaphoreType.REGULAR,
         ],
         compiler_params=pltpu.CompilerParams(
             collective_id=0, has_side_effects=True, vmem_limit_bytes=60 * 1024 * 1024

time: 60.5 us -> 61.1 us (level)
  no operation moved by 1% of the time
where the time goes in v7:
time: 61.1 us; the launch traced here: 60.9 us
  Pallas kernels  59.5 us (97%)
  other arithmetic  0.72 us (1%)
  between operations  0.67 us (1%)
    pallas_call x1, Pallas kernels, on_device(): pl.pallas_call(kernel, out_shape=pltpu.VMEM((1, rows, width), F32), in_sp...  59.5 us

profile of v7, /device:TPU:1, one launch (start us, length us, event | category | flops | bytes accessed | tf_op | source)
XLA Modules:
  0.0 60.9 jit_solution(15667919787222868576)
XLA Ops:
  0.7 59.5 %sector_step.1 = f32[1,32,512]{2,1,0:T(8,128)S(1)} custom-call(bf16[1,32,512]{2,1,0:T(8,128)(2,1)} %state.1, bf16[16,32,512]{2,1,0:T(8,128)(2,1)} %bitcast.11, bf16[72,32,512]{2,1,0:T(8,128)(2,1)} %left.1, bf16[1,72]{1,0:T(2,128)(2,1)} %bitcast.12, s32[1,72]{1,0:T(1,128)} %bitcast.13, s32[1,72]{1,0:T(1,128)} %bitcast.14, s32[1,1]{1,0:T(1,128)} %bitcast.10.dims), custom_call_target="tpu_custom_call" | custom-call | tf_op jit(solution)/shard_map/sector_step/pallas_call | solution.py:592
  60.2 0.7 %and_select_fusion = f32[1,32,512]{2,1,0:T(8,128)} fusion(f32[1,32,512]{2,1,0:T(8,128)S(1)} %sector_step.1, pred[512]{0:T(512)(128)(4,1)S(1)} %iota_compare_fusion, pred[32]{0:T(512)(128)(4,1)S(1)} %add_compare_fusion), kind=kLoop, calls=%fused_computation | loop fusion | flops 32768 | bytes 131616 | tf_op jit(solution)/shard_map/jit(_where)/select_n | solution.py:654
  (2 shorter events, 0.0 us)
